TPU v7x, 32 devices: a whole 2x2x4 slice. The times are simulated.
32 devices in a mesh: grp: 4 (over z), hap: 8 (over y, x, core).
Axes of the slice: x: 2, y: 2, z: 4, core: 2. Of those that a mesh axis runs over, the one named last changes fastest.
Arguments:
- alleles: int32 [60, 512], P('grp', 'hap'), may hold values from 0 to 1073741823
- observed: int32 [60, 32], P('grp', 'hap'), may hold values from 0 to 2
- map_steps: int32 [60], P('grp'), may hold values from 1 to 99
- start_weights: float32 [32, 15360], P('hap'), may hold values from 1e-12 to 1
- end_weights: float32 [32, 15360], P('hap'), may hold values from 1e-12 to 1
Outputs:
- dosage: float32 [60, 32], P('grp', 'hap')
Inputs may be any that keep to these rules, and one draw needn't show every extreme that they name: Bit b of alleles[m, w] is the allele 0 or 1 of reference haplotype 30 w + b at marker m. 0 and 1 are observed alleles, 2 marks a marker not typed in that target.
All inputs are finite; a program needn't handle non-finite values.
Results may differ from a plain program's by a relative error of at most 0.0008.
Values sent between devices are 32-bit elements; how exact they have to be, the bound alone decides.
A program may use at most 128 MiB of HBM per device.

v0:
```python
import functools
import jax
import jax.numpy as jnp
from jax import lax
from jax.experimental import pallas as pl
from jax.experimental.pallas import tpu as pltpu
from jax.sharding import PartitionSpec as P

error_rate = 0.01
map_unit = 100000.0
SUB, LANE = 8, 128
MESH = pl.DeviceIdType.MESH


def total(parts):
    parts = list(parts)
    while len(parts) > 1:
        parts = [a + b for a, b in zip(parts[::2], parts[1::2])] + parts[len(parts) // 2 * 2:]
    return parts[0]


def block_size(local_m):
    return next(n for n in (5, 4, 3, 2, 1) if local_m % n == 0)


def whole_sum(parts):
    return jnp.sum(total(parts), keepdims=True)


def kernel(dims, alleles, observed, steps, starts, ends, out, tmp, meta, sbuf, recv, recv_meta,
           bits, table, staged, fstore, bstore, emit, runs, numer, denom, dos, out_recv,
           start_rows, end_rows, weight_sem, send_sem, recv_sem, meta_send, meta_recv, out_send, out_recv_sem):
    groups, haps, local_m, targets, words, bits_word = dims
    total_haps = words * bits_word
    local_w = words // haps
    span = words // SUB
    reps = LANE // span
    vecs = bits_word // reps
    pack = LANE // local_w
    rows = -(-local_m // pack)
    slots = pack * rows
    share = haps // SUB
    half = groups // 2
    size = block_size(local_m)
    g_me, h_me = lax.axis_index("grp"), lax.axis_index("hap")
    devices = groups * haps
    mine = lax.rem(g_me, targets)

    weight_copies = [
        pltpu.make_async_copy(source, target, weight_sem.at[n])
        for n, (source, target) in enumerate([(starts, start_rows), (ends, end_rows)])
    ]
    for copy in weight_copies:
        copy.start()

    def each_peer(act):
        def visit(k, d):
            g = jnp.where(g_me < half, groups - 1 - k, k)
            h = lax.rem(h_me + d, haps)
            if isinstance(d, int) and d:
                act(g, h)
            else:
                pl.when((g != g_me) | (h != h_me))(lambda: act(g, h))

        if devices <= 64:
            for k in range(groups):
                for d in range(haps):
                    visit(k, d)
        else:
            @pl.loop(0, groups)
            def _(k):
                pl.loop(0, haps)(functools.partial(visit, k))

    barrier = pltpu.get_barrier_semaphore()
    each_peer(lambda g, h: pl.semaphore_signal(barrier, inc=1, device_id=(g, h), device_id_type=MESH))

    lane = lax.broadcasted_iota(jnp.int32, (SUB, LANE), 1)
    tmp[...] = jnp.zeros_like(tmp)
    tmp[0:local_m, 0:local_w] = alleles[...]
    dense = tmp[0:SUB, :]
    for p in range(1, pack):
        dense = jnp.where(lane // local_w == p, pltpu.roll(tmp[p * rows:p * rows + SUB, :], p * local_w, 1), dense)
    sbuf[...] = dense
    recv[g_me, pl.ds(pl.multiple_of(h_me * SUB, SUB), SUB), :] = dense
    meta[...] = jnp.zeros_like(meta)
    meta[0:targets, 0:local_m] = observed[...]
    columns = meta[...]
    sub_at = lax.broadcasted_iota(jnp.int32, (SUB, LANE), 0)
    for i in range(local_m):
        columns = jnp.where((sub_at == targets) & (lane == i), steps[i], columns)
    meta[...] = columns
    recv_meta[g_me] = columns

    def arrange(weights):
        for r in range(vecs):
            for s in range(SUB):
                at = s * vecs + r
                staged[at * targets:(at + 1) * targets, :] = weights[:, at * LANE:(at + 1) * LANE]
        source = [staged[pl.ds(r * targets + mine, SUB, stride=vecs * targets), :] for r in range(vecs)]
        result = []
        for q in range(vecs):
            spot = bits_word * (lane % span) + reps * q + lane // span
            chosen, within = spot // LANE, spot % LANE
            value = jnp.zeros((SUB, LANE), jnp.float32)
            for r in range(vecs):
                moved = jnp.take_along_axis(source[r], within, axis=1, mode="promise_in_bounds")
                value = jnp.where(chosen == r, moved, value)
            result.append(value)
        inverse = 1.0 / whole_sum(result)
        return [value * inverse for value in result]

    weight_copies[0].wait()
    fwd = arrange(start_rows)

    pl.semaphore_wait(barrier, devices - 1)

    def block_copy(g, h, sem_g, sem_h):
        return pltpu.make_async_remote_copy(
            src_ref=sbuf, dst_ref=recv.at[sem_g, pl.ds(pl.multiple_of(sem_h * SUB, SUB), SUB), :],
            send_sem=send_sem.at[g, h], recv_sem=recv_sem.at[sem_g, sem_h],
            device_id=(g, h), device_id_type=MESH)

    def meta_copy(g, sem_g):
        return pltpu.make_async_remote_copy(
            src_ref=meta, dst_ref=recv_meta.at[sem_g], send_sem=meta_send.at[g], recv_sem=meta_recv.at[sem_g],
            device_id=(g, h_me), device_id_type=MESH)

    @pl.loop(1, groups)
    def _(d):
        g = lax.rem(g_me + d, groups)
        meta_copy(g, g_me).start()

    def send_blocks():
        each_peer(lambda g, h: block_copy(g, h, g_me, h_me).start())

    outer = (g_me == 0) | (g_me == groups - 1)
    pl.when(outer)(send_blocks)
    weight_copies[1].wait()
    bwd = arrange(end_rows)
    pl.when(jnp.logical_not(outer))(send_blocks)

    @pl.loop(1, groups)
    def _(d):
        meta_copy(g_me, lax.rem(g_me + d, groups)).wait_recv()

    @pl.loop(0, groups)
    def _(g):
        entry = recv_meta.at[g]
        same = lax.broadcasted_iota(jnp.int32, (slots, LANE), 0) == lax.broadcasted_iota(jnp.int32, (slots, LANE), 1)

        def turned(at):
            values = jnp.broadcast_to(entry[pl.ds(at, 1), :].astype(jnp.float32), (slots, LANE))
            summed = jnp.sum(jnp.where(same, values, 0.0), axis=1, keepdims=True)
            return jnp.broadcast_to(summed, (slots, LANE))

        seen, dist = turned(mine), turned(targets)
        rate = 1.0 - jnp.exp(-dist / map_unit)
        at = pl.ds(pl.multiple_of(g * slots, SUB), slots)
        table[0, at, :] = jnp.where(seen == 2.0, 1.0, jnp.where(seen == 1.0, 1.0 - error_rate, error_rate))
        table[1, at, :] = jnp.where(seen == 2.0, 1.0, jnp.where(seen == 0.0, 1.0 - error_rate, error_rate))
        table[2, at, :] = 1.0 - rate
        table[3, at, :] = rate / total_haps

    def expand(g):
        @pl.loop(0, haps)
        def _(h):
            @pl.when((g != g_me) | (h != h_me))
            def _():
                block_copy(g_me, h_me, g, h).wait_recv()

        for r in range(rows):
            loads = [recv[g, pl.ds(j * SUB + r, SUB, stride=SUB * share), :] for j in range(share)]
            for p in range(pack):
                value = jnp.zeros((SUB, LANE), jnp.int32)
                for e in range(reps):
                    for j in range(share):
                        begin = e * span + j * local_w
                        shift = (begin - p * local_w) % LANE
                        piece = loads[j] if shift == 0 else pltpu.roll(loads[j], shift, 1)
                        piece = piece if e == 0 else jnp.right_shift(piece, e)
                        value = jnp.where((lane >= begin) & (lane < begin + local_w), piece, value)
                bits[g * slots + p * rows + r] = value

    def row(kind, slot):
        return jnp.broadcast_to(table[kind, pl.ds(slot, 1), :], (SUB, LANE))

    def add_up(value):
        for shift in (4, 2, 1):
            value = value + pltpu.roll(value, shift, 0)
        return jnp.broadcast_to(jnp.sum(value, axis=1, keepdims=True), (SUB, LANE))

    pairs = [(j, i) for j in range(size) for i in range(j, size)]

    def spans(slot, block):
        sums = {pair: [] for pair in pairs}
        words_in = [bits[slot + i] for i in range(size)]
        tops = [(row(0, slot + i), row(1, slot + i)) for i in range(size)]
        for q in range(vecs):
            e = [jnp.where(jnp.bitwise_and(words_in[i], 1 << (reps * q)) != 0, *tops[i]) for i in range(size)]
            for i in range(size):
                emit[slot + i, q] = e[i]
            for j in range(size):
                run = e[j]
                for i in range(j, size):
                    run = run if i == j else run * e[i]
                    sums[j, i] = [run] if q == 0 else [sums[j, i][0] + run]
        result = {}
        for at, pair in enumerate(pairs):
            result[pair] = add_up(sums[pair][0])
            runs[block, at] = result[pair]
        return result

    def kept_spans(block):
        return {pair: runs[block, at] for at, pair in enumerate(pairs)}

    def ahead(state, order):
        sums = [None] * size
        for q in range(vecs):
            value = state[q]
            for i, slot in enumerate(order):
                value = value * emit[slot, q]
                sums[i] = value if q == 0 else sums[i] + value
        return [add_up(value) for value in sums]

    def solve_forward(first, span, order):
        keep = [row(2, slot) for slot in order]
        add = [row(3, slot) for slot in order]
        sums, terms = [], []
        lead = None
        for i in range(size):
            lead = keep[i] if i == 0 else lead * keep[i]
            terms = [term * keep[i] for term in terms]
            terms.append(add[i] if i == 0 else add[i] * sums[i - 1])
            value = lead * first[i]
            for j, term in enumerate(terms):
                value = value + term * span[j, i]
            sums.append(value)
        scale = [(1.0 if i == 0 else sums[i - 1]) / sums[i] for i in range(size)]
        return [keep[i] * scale[i] for i in range(size)], [add[i] * scale[i] for i in range(size)]

    def solve_backward(first, span, order):
        keep = [row(2, slot) for slot in order]
        add = [row(3, slot) for slot in order]
        sums, terms = [], []
        lead = None
        for i in range(size):
            value = first[i] if i == 0 else lead * first[i]
            for j, term in enumerate(terms):
                value = value + term * span[size - 1 - i, size - 2 - j]
            sums.append(value)
            lead = keep[i] if i == 0 else lead * keep[i]
            terms = [term * keep[i] for term in terms] + [add[i] * value]
        scale = [(1.0 if i == 0 else sums[i - 1]) / sums[i] for i in range(size)]
        return [keep[i] * scale[i] for i in range(size)], add

    blocks = local_m // size

    def place(s, n):
        slot = s * slots + n * size
        return slot, s * local_m + n * size, s * blocks + n

    def store_section(s, carry):
        expand(s)
        expand(groups - 1 - s)

        def step(n, carry):
            f, b = list(carry[:vecs]), list(carry[vecs:])
            fs, fm, fb = place(s, n)
            bs, _, bb = place(groups - 1 - s, blocks - 1 - n)
            bm = s * local_m + n * size
            f_order = [fs + i for i in range(size)]
            b_order = [bs + size - 1 - i for i in range(size)]
            f_span, b_span = spans(fs, fb), spans(bs, bb)
            f_first, b_first = ahead(f, f_order), ahead(b, b_order)
            f_keep, f_add = solve_forward(f_first, f_span, f_order)
            b_keep, b_add = solve_backward(b_first, b_span, b_order)
            for q in range(vecs):
                for i in range(size):
                    f[q] = emit[f_order[i], q] * (f_keep[i] * f[q] + f_add[i])
                    fstore[fm + i, q] = f[q]
                    bstore[bm + i, q] = b[q]
                    b[q] = b_keep[i] * (emit[b_order[i], q] * b[q]) + b_add[i]
            return tuple(f) + tuple(b)

        return lax.fori_loop(0, blocks, step, carry)

    def half_type(value):
        return value.astype(jnp.bfloat16).astype(jnp.float32)

    def out_copy(g, owner):
        return pltpu.make_async_remote_copy(
            src_ref=dos.at[g], dst_ref=out_recv.at[owner], send_sem=out_send.at[g],
            recv_sem=out_recv_sem.at[owner], device_id=(g, h_me), device_id_type=MESH)

    owner = g_me < targets

    def finish(*finished):
        for g in finished:
            at = pl.ds(g * slots, local_m)
            top = jnp.sum(jnp.sum(numer[at], axis=1), axis=1, keepdims=True)
            low = jnp.sum(jnp.sum(denom[at], axis=1), axis=1, keepdims=True)
            dos[g, 0:local_m, :] = jnp.broadcast_to(top / low, (local_m, LANE))
        for g in finished:
            pl.when((g != g_me) & owner)(out_copy(g, g_me).start)

    def score_section(s, carry):
        def step(n, carry):
            f, b = list(carry[:vecs]), list(carry[vecs:])
            fs, _, fb = place(s, n)
            bs, _, bb = place(groups - 1 - s, blocks - 1 - n)
            other = (groups - 1 - s) * local_m + local_m - 1 - n * size
            f_order = [fs + i for i in range(size)]
            b_order = [bs + size - 1 - i for i in range(size)]
            f_first, b_first = ahead(f, f_order), ahead(b, b_order)
            f_keep, f_add = solve_forward(f_first, kept_spans(fb), f_order)
            b_keep, b_add = solve_backward(b_first, kept_spans(bb), b_order)
            tops, lows = {}, {}

            def score(key, q, x, y, slot):
                prod = half_type(x) * half_type(y)
                part = jnp.where(jnp.bitwise_and(bits[slot], 1 << (reps * q)) != 0, prod, 0.0)
                tops[key] = part if q == 0 else tops[key] + part
                lows[key] = prod if q == 0 else lows[key] + prod

            for q in range(vecs):
                for i in range(size):
                    f[q] = emit[f_order[i], q] * (f_keep[i] * f[q] + f_add[i])
                    score((0, i), q, f[q], bstore[other - i, q], f_order[i])
                    score((1, i), q, fstore[other - i, q], b[q], b_order[i])
                    b[q] = b_keep[i] * (emit[b_order[i], q] * b[q]) + b_add[i]
            for i in range(size):
                numer[f_order[i]], denom[f_order[i]] = tops[0, i], lows[0, i]
                numer[b_order[i]], denom[b_order[i]] = tops[1, i], lows[1, i]
            return tuple(f) + tuple(b)

        carry = lax.fori_loop(0, blocks, step, carry)
        finish(s, groups - 1 - s)
        return carry

    carry = lax.fori_loop(0, half, store_section, tuple(fwd) + tuple(bwd))
    lax.fori_loop(half, groups, score_section, carry)

    @pl.loop(1, groups)
    def _(d):
        meta_copy(lax.rem(g_me + d, groups), g_me).wait_send()

    each_peer(lambda g, h: block_copy(g, h, g_me, h_me).wait_send())

    @pl.when(owner)
    def _():
        out_recv[g_me, 0:local_m, :] = dos[g_me, 0:local_m, :]

    @pl.loop(0, targets)
    def _(t):
        @pl.when(t != g_me)
        def _():
            out_copy(g_me, t).wait_recv()

    lane_m = lax.broadcasted_iota(jnp.int32, (local_m, LANE), 1)
    result = jnp.zeros((local_m, LANE), jnp.float32)
    for t in range(targets):
        result = jnp.where(lane_m == t, out_recv[t, 0:local_m, :], result)
    out[...] = result[:, 0:targets]

    @pl.when(owner)
    def _():
        @pl.loop(1, groups)
        def _(d):
            out_copy(lax.rem(g_me + d, groups), g_me).wait_send()


def solution(mesh):
    groups, haps = mesh.shape["grp"], mesh.shape["hap"]

    def local(alleles, observed, map_steps, start_weights, end_weights):
        local_m, local_w = alleles.shape
        targets, total_haps = start_weights.shape
        words = local_w * haps
        bits_word = total_haps // words
        reps = LANE * SUB // words
        vecs = bits_word // reps
        pack = LANE // local_w
        slots = pack * -(-local_m // pack)
        markers = local_m * groups
        size = block_size(local_m)
        assert targets < SUB and targets <= groups and groups % 2 == 0 and slots % SUB == 0
        vmem = pl.BlockSpec(memory_space=pltpu.VMEM)
        dims = (groups, haps, local_m, targets, words, bits_word)
        f32, i32 = jnp.float32, jnp.int32
        dma = pltpu.SemaphoreType.DMA
        return pl.pallas_call(
            functools.partial(kernel, dims),
            out_shape=jax.ShapeDtypeStruct((local_m, targets), f32),
            in_specs=[vmem, vmem, pl.BlockSpec(memory_space=pltpu.SMEM)] + [pl.BlockSpec(memory_space=pltpu.HBM)] * 2,
            out_specs=vmem,
            scratch_shapes=[
                pltpu.VMEM((slots + SUB, LANE), i32),
                pltpu.VMEM((SUB, LANE), i32),
                pltpu.VMEM((SUB, LANE), i32),
                pltpu.VMEM((groups, haps * SUB, LANE), i32),
                pltpu.VMEM((groups, SUB, LANE), i32),
                pltpu.VMEM((groups * slots, SUB, LANE), i32),
                pltpu.VMEM((4, groups * slots, LANE), f32),
                pltpu.VMEM((vecs * SUB * targets, LANE), f32),
                pltpu.VMEM((markers // 2, vecs, SUB, LANE), f32),
                pltpu.VMEM((markers // 2, vecs, SUB, LANE), f32),
                pltpu.VMEM((groups * slots, vecs, SUB, LANE), f32),
                pltpu.VMEM((markers // size, size * (size + 1) // 2, SUB, LANE), f32),
                pltpu.VMEM((groups * slots, SUB, LANE), f32),
                pltpu.VMEM((groups * slots, SUB, LANE), f32),
                pltpu.VMEM((groups, slots, LANE), f32),
                pltpu.VMEM((targets, slots, LANE), f32),
                pltpu.VMEM((targets, total_haps), f32), pltpu.VMEM((targets, total_haps), f32), dma((2,)),
                dma((groups, haps)), dma((groups, haps)),
                dma((groups,)), dma((groups,)), dma((groups,)), dma((targets,)),
            ],
            compiler_params=pltpu.CompilerParams(
                collective_id=0, has_side_effects=True, vmem_limit_bytes=60 * 1024 * 1024),
        )(alleles, observed.T, map_steps, start_weights, end_weights)

    in_specs = (P("grp", "hap"), P("grp", "hap"), P("grp"), P("hap", None), P("hap", None))
    return jax.shard_map(local, mesh=mesh, in_specs=in_specs, out_specs=P("grp", "hap"), check_vma=False)
```

profile of v0, /device:TPU:0, one launch (start us, length us, event | category | flops | bytes accessed | tf_op | source)
XLA Modules:
  0.0 23.7 jit_solution(3440674338377870949)
XLA Ops:
  0.0 22.3 %shard_map.55 = f32[15,4]{1,0:T(8,128)} custom-call(s32[15,64]{1,0:T(8,128)} %alleles.1, s32[4,15]{1,0:T(4,128)} %bitcast.1, s32[15]{0:T(128)} %steps.1, f32[4,15360]{1,0:T(4,128)} %starts.1, f32[4,15360]{1,0:T(4,128)} %ends.1), custom_call_target="tpu_custom_call" | custom-call | tf_op jit(solution)/shard_map/pallas_call | solution.py:391
  22.4 1.4 %copy.6 = f32[15,4]{0,1:T(4,128)} copy(f32[15,4]{1,0:T(8,128)} %shard_map.55) | data formatting | bytes 480 | tf_op jit(solution)/shard_map/pallas_call | solution.py:391
where the time goes:
time: 24 us; the launch traced here: 23.7 us
  Pallas kernels  22.3 us (93%)
  local copies, waits for them, and re-layouts  1.35 us (6%)
    pallas_call x1, Pallas kernels, local(): pl.pallas_call(functools.partial(kernel, dims), out_shape=jax.ShapeDtypeS...  22.3 us
    pallas_call x1, local copies, waits for them, and re-layouts, local(): pl.pallas_call(functools.partial(kernel, dims), out_shape=jax.ShapeDtypeS...  1.35 us

commit v1 on v0

v1 whole, which is shorter than its diff:
```python
import functools
import jax
import jax.numpy as jnp
from jax import lax
from jax.experimental import pallas as pl
from jax.experimental.pallas import tpu as pltpu
from jax.sharding import PartitionSpec as P

error_rate = 0.01
map_unit = 100000.0
SUB, LANE = 8, 128
MESH = pl.DeviceIdType.MESH


def total(parts):
    parts = list(parts)
    while len(parts) > 1:
        parts = [a + b for a, b in zip(parts[::2], parts[1::2])] + parts[len(parts) // 2 * 2:]
    return parts[0]


def block_size(local_m):
    return next(n for n in (5, 4, 3, 2, 1) if local_m % n == 0)


def kernel(dims, alleles, observed, steps, starts, ends, out,
           own_alleles, own_observed, own_steps, tmp, col, recv, bits, table, weights, staged,
           state_a, state_b, emit, runs, kept, kept_low, waiting, numer, denom, dos, out_recv,
           load_sem, z_send, z_recv, p_send, p_recv, out_send, out_recv_sem):
    groups, haps, local_m, targets, words, bits_word = dims
    total_haps = words * bits_word
    local_w = words // haps
    span = words // SUB
    reps = LANE // span
    vecs = bits_word // reps
    pack = LANE // local_w
    rows = -(-local_m // pack)
    slots = pack * rows
    share = haps // SUB
    half = groups // 2
    size = block_size(local_m)
    blocks = local_m // size
    end_row = groups * slots
    g_me, h_me = lax.axis_index("grp"), lax.axis_index("hap")
    mine = lax.rem(g_me, targets)
    near = g_me < half

    loads = [
        pltpu.make_async_copy(source, target, load_sem.at[n]) for n, (source, target) in enumerate([
            (alleles, own_alleles), (observed, own_observed), (steps, own_steps),
            (starts, weights.at[0]), (ends, weights.at[1])])
    ]
    for load in loads:
        load.start()

    def each_hap(act):
        if haps <= 8:
            for d in range(1, haps):
                act(lax.rem(h_me + d, haps))
        else:
            pl.loop(1, haps)(lambda d: act(lax.rem(h_me + d, haps)))

    def each_group_step(act):
        if groups <= 4:
            for d in range(1, groups):
                act(d)
        else:
            pl.loop(1, groups)(act)

    barrier = pltpu.get_barrier_semaphore()

    def greet(g, h):
        pl.semaphore_signal(barrier, inc=1, device_id=(g, h), device_id_type=MESH)

    pl.when(g_me > 0)(lambda: greet(g_me - 1, h_me))
    each_group_step(lambda d: pl.when(g_me + d < groups)(lambda: greet(g_me + d, h_me)))
    each_hap(lambda h: greet(g_me, h))

    lane = lax.broadcasted_iota(jnp.int32, (SUB, LANE), 1)
    sub_at = lax.broadcasted_iota(jnp.int32, (SUB, LANE), 0)
    tmp[...] = jnp.zeros_like(tmp)
    for load in loads[:3]:
        load.wait()
    tmp[0:local_m, 0:local_w] = own_alleles[...]
    dense = tmp[0:SUB, :]
    for p in range(1, pack):
        dense = jnp.where(lane // local_w == p, pltpu.roll(tmp[p * rows:p * rows + SUB, :], p * local_w, 1), dense)
    col[g_me, 0:SUB, :] = dense
    recv[g_me, pl.ds(pl.multiple_of(h_me * SUB, SUB), SUB), :] = dense
    tmp[0:targets, 0:local_m] = own_observed[...]
    columns = tmp[0:SUB, :]
    for i in range(local_m):
        columns = jnp.where((sub_at == targets) & (lane == i), own_steps[i], columns)
    col[g_me, SUB:2 * SUB, :] = columns

    def z_copy(block, g):
        return pltpu.make_async_remote_copy(
            src_ref=col.at[block], dst_ref=col.at[block], send_sem=z_send.at[block, g], recv_sem=z_recv.at[block],
            device_id=(g, h_me), device_id_type=MESH)

    def p_copy(block, h, sem_h):
        return pltpu.make_async_remote_copy(
            src_ref=col.at[block, 0:SUB], dst_ref=recv.at[block, pl.ds(pl.multiple_of(sem_h * SUB, SUB), SUB), :],
            send_sem=p_send.at[block, h], recv_sem=p_recv.at[block, sem_h],
            device_id=(g_me, h), device_id_type=MESH)

    def spread(block):
        each_hap(lambda h: p_copy(block, h, h_me).start())

    def each_z_copy(act):
        pl.when(g_me + 1 < groups)(lambda: act(z_copy(g_me, g_me + 1)))
        each_group_step(lambda d: pl.when(g_me - d >= 0)(lambda: act(z_copy(g_me, g_me - d))))

    pl.semaphore_wait(barrier, g_me + jnp.where(g_me < groups - 1, 1, 0) + haps - 1)
    each_z_copy(lambda copy: copy.start())
    spread(g_me)

    def arrange(which, state):
        source_rows = weights.at[which]
        for r in range(vecs):
            for s in range(SUB):
                at = s * vecs + r
                staged[at * targets:(at + 1) * targets, :] = source_rows[:, at * LANE:(at + 1) * LANE]
        source = [staged[pl.ds(r * targets + mine, SUB, stride=vecs * targets), :] for r in range(vecs)]
        result = []
        for q in range(vecs):
            spot = bits_word * (lane % span) + reps * q + lane // span
            chosen, within = spot // LANE, spot % LANE
            value = jnp.zeros((SUB, LANE), jnp.float32)
            for r in range(vecs):
                moved = jnp.take_along_axis(source[r], within, axis=1, mode="promise_in_bounds")
                value = jnp.where(chosen == r, moved, value)
            state[q] = value
            result.append(value)
        return 1.0 / add_up(total(result))

    def add_up(value):
        for shift in (4, 2, 1):
            value = value + pltpu.roll(value, shift, 0)
        return jnp.broadcast_to(jnp.sum(value, axis=1, keepdims=True), (SUB, LANE))

    for load in loads[3:]:
        load.wait()
    scale_a = arrange(jnp.where(near, 0, 1), state_a)

    def arrived(block):
        z_copy(block, g_me).wait_recv()

    def keep_own(block):
        recv[block, pl.ds(pl.multiple_of(h_me * SUB, SUB), SUB), :] = col[block, 0:SUB, :]

    def relay(d):
        low, high = g_me - d, g_me + d

        @pl.when(low >= 0)
        def _():
            arrived(low)
            pl.when(g_me + 1 < groups)(z_copy(low, g_me + 1).start)
            spread(low)
            keep_own(low)

        @pl.when(high < groups)
        def _():
            arrived(high)
            spread(high)
            keep_own(high)

    if groups <= 4:
        relay(1)
        scale_b = arrange(jnp.where(near, 1, 0), state_b)
        for d in range(2, groups):
            relay(d)
    else:
        scale_b = arrange(jnp.where(near, 1, 0), state_b)
        pl.loop(1, groups)(relay)

    table[2, end_row:end_row + SUB, :] = jnp.zeros((SUB, LANE), jnp.float32)

    @pl.loop(0, groups)
    def _(g):
        same = lax.broadcasted_iota(jnp.int32, (slots, LANE), 0) == lax.broadcasted_iota(jnp.int32, (slots, LANE), 1)

        def turned(at):
            values = jnp.broadcast_to(col[g, pl.ds(SUB + at, 1), :].astype(jnp.float32), (slots, LANE))
            summed = jnp.sum(jnp.where(same, values, 0.0), axis=1, keepdims=True)
            return jnp.broadcast_to(summed, (slots, LANE))

        seen, dist = turned(mine), turned(targets)
        rate = 1.0 - jnp.exp(-dist / map_unit)
        at = pl.ds(pl.multiple_of(g * slots, SUB), slots)
        table[0, at, :] = jnp.where(seen == 2.0, 1.0, jnp.where(seen == 1.0, 1.0 - error_rate, error_rate))
        table[1, at, :] = jnp.where(seen == 2.0, 1.0, jnp.where(seen == 0.0, 1.0 - error_rate, error_rate))
        table[2, at, :] = (rate / total_haps) / (1.0 - rate)

    def group_at(s):
        return jnp.where(near, s, groups - 1 - s)

    def marker_at(n):
        return jnp.where(near, n, local_m - 1 - n)

    def expand(s):
        g = group_at(s)
        each_hap(lambda h: p_copy(g, h, h).wait_recv())
        for r in range(rows):
            parts = [recv[g, pl.ds(j * SUB + r, SUB, stride=SUB * share), :] for j in range(share)]
            for p in range(pack):
                n = p * rows + r
                if n >= local_m:
                    continue
                value = jnp.zeros((SUB, LANE), jnp.int32)
                for e in range(reps):
                    for j in range(share):
                        begin = e * span + j * local_w
                        shift = (begin - p * local_w) % LANE
                        piece = parts[j] if shift == 0 else pltpu.roll(parts[j], shift, 1)
                        piece = piece if e == 0 else jnp.right_shift(piece, e)
                        value = jnp.where((lane >= begin) & (lane < begin + local_w), piece, value)
                bits[s * slots + marker_at(n)] = value

    def row(kind, slot):
        return jnp.broadcast_to(table[kind, pl.ds(slot, 1), :], (SUB, LANE))

    def share_rows(s, n):
        g, at = group_at(s), marker_at(n)
        this = g * slots + at
        after = jnp.where(at + 1 < local_m, this + 1, jnp.where(g + 1 < groups, (g + 1) * slots, end_row))
        return jnp.where(near, this, after), jnp.where(near, after, this)

    def masked(words_in, q):
        return jnp.bitwise_and(words_in, 1 << (reps * q)) != 0

    pairs = [(j, i) for j in range(size) for i in range(j, size)]

    def prepare(s, n):
        at = s * slots + n * size
        sums = {}
        words_in = [bits[at + i] for i in range(size)]
        tops = []
        for i in range(size):
            slot = group_at(s) * slots + marker_at(n * size + i)
            tops.append((row(0, slot), row(1, slot)))
        for q in range(vecs):
            e = [jnp.where(masked(words_in[i], q), *tops[i]) for i in range(size)]
            for i in range(size):
                emit[at + i, q] = e[i]
            for j in range(size):
                run = e[j]
                for i in range(j, size):
                    run = run if i == j else run * e[i]
                    sums[j, i] = run if q == 0 else sums[j, i] + run
        for k, pair in enumerate(pairs):
            runs[s * blocks + n, k] = add_up(sums[pair])

    def solve(state, scale, s, n, order, which):
        at = s * slots + n * size
        sums = [None] * size
        for q in range(vecs):
            value = state[q]
            for i in order:
                value = value * emit[at + i, q]
                sums[i] = value if q == 0 else sums[i] + value
        span_of = {pair: runs[s * blocks + n, k] for k, pair in enumerate(pairs)}
        adds = {}
        last = None
        for i in order:
            share_of = row(2, share_rows(s, n * size + i)[which])
            adds[i] = share_of if last is None else share_of * last
            last = add_up(sums[i]) * scale
            for j in adds:
                last = last + adds[j] * span_of[min(i, j), max(i, j)]
        return adds, 1.0 / last

    up, down = list(range(size)), list(range(size))[::-1]

    def step_a(s, n, scale):
        at = s * slots + n * size
        adds, after = solve(state_a, scale, s, n, up, 0)
        words_in = [bits[at + i] for i in range(size)]
        for q in range(vecs):
            value = state_a[q] * scale
            for i in up:
                value = emit[at + i, q] * (value + adds[i])
                kept[at + i, q] = jnp.where(masked(words_in[i], q), value, 0.0)
            kept_low[s * blocks + n, q] = value
            state_a[q] = value
        return after

    def put_sums(s, n, tops, low):
        for i in range(size):
            at = pl.ds(pl.multiple_of((s * slots + n * size + i) * SUB, SUB), SUB)
            numer[at, :] = tops[i]
            denom[at, :] = low

    def step_b(s, n, scale, score):
        at = s * slots + n * size
        adds, after = solve(state_b, scale, s, n, down, 1)
        tops, low = [None] * size, None
        for q in range(vecs):
            value = state_b[q] * scale
            for i in down:
                value = value + adds[i]
                if score:
                    part = kept[at + i, q] * value
                    tops[i] = part if q == 0 else tops[i] + part
                    if i == size - 1:
                        part = kept_low[s * blocks + n, q] * value
                        low = part if q == 0 else low + part
                else:
                    waiting[n * size + i, q] = value
                value = emit[at + i, q] * value
            state_b[q] = value
        if score:
            put_sums(s, n, tops, low)
        return after

    def score_waiting(s, n):
        at = s * slots + n * size
        tops = [total(kept[at + i, q] * waiting[n * size + i, q] for q in range(vecs)) for i in range(size)]
        last = n * size + size - 1
        put_sums(s, n, tops, total(kept_low[s * blocks + n, q] * waiting[last, q] for q in range(vecs)))

    owner = g_me < targets

    def out_copy(g, target):
        return pltpu.make_async_remote_copy(
            src_ref=dos.at[g], dst_ref=out_recv.at[target], send_sem=out_send.at[g],
            recv_sem=out_recv_sem.at[target], device_id=(g, h_me), device_id_type=MESH)

    row_at = lax.broadcasted_iota(jnp.int32, (slots, LANE), 0)
    own_lane = lax.broadcasted_iota(jnp.int32, (slots, LANE), 1) == jnp.where(near, row_at, local_m - 1 - row_at)

    def finish(s):
        g = group_at(s)

        def gathered(sums):
            parts = [sums[pl.ds(s * slots * SUB + k, slots, stride=SUB), :] for k in range(SUB)]
            return jnp.sum(total(parts), axis=1, keepdims=True)

        value = jnp.broadcast_to(gathered(numer) / gathered(denom), (slots, LANE))
        value = jnp.where(own_lane & (row_at < local_m), value, 0.0)
        dos[g] = jnp.broadcast_to(jnp.sum(value, axis=0, keepdims=True), (SUB, LANE))
        pl.when((g != g_me) & owner)(lambda: out_copy(g, g_me).start())

    def first_pass(s, scale):
        expand(s)
        for n in range(blocks):
            prepare(s, n)
            scale = step_a(s, n, scale)
        return scale

    far = groups - 1
    scale_a = lax.fori_loop(0, far, first_pass, scale_a)
    expand(far)
    ready = set()
    for n in range(blocks):
        for k in (n, blocks - 1 - n):
            if k not in ready:
                ready.add(k)
                prepare(far, k)
        scale_a = step_a(far, n, scale_a)
        scale_b = step_b(far, blocks - 1 - n, scale_b, False)
    for n in range(blocks):
        score_waiting(far, n)

    def second_pass(k, scale):
        s = far - 1 - k
        finish(s + 1)
        for n in reversed(range(blocks)):
            scale = step_b(s, n, scale, True)
        return scale

    lax.fori_loop(0, far, second_pass, scale_b)
    finish(0)

    each_z_copy(lambda copy: copy.wait_send())
    each_hap(lambda h: p_copy(g_me, h, h_me).wait_send())

    def drain(d):
        low, high = g_me - d, g_me + d

        @pl.when(low >= 0)
        def _():
            pl.when(g_me + 1 < groups)(lambda: z_copy(low, g_me + 1).wait_send())
            each_hap(lambda h: p_copy(low, h, h_me).wait_send())

        @pl.when(high < groups)
        def _():
            each_hap(lambda h: p_copy(high, h, h_me).wait_send())

    each_group_step(drain)

    @pl.when(owner)
    def _():
        out_recv[g_me] = dos[g_me]
        each_group_step(lambda d: out_copy(lax.rem(g_me + d, groups), g_me).wait_send())

    @pl.loop(0, targets)
    def _(t):
        pl.when(t != g_me)(lambda: out_copy(g_me, t).wait_recv())

    result = out_recv[0]
    for t in range(1, targets):
        result = jnp.where(sub_at == t, out_recv[t], result)
    out[...] = result[0:targets, 0:local_m]


def solution(mesh):
    groups, haps = mesh.shape["grp"], mesh.shape["hap"]

    def local(alleles, observed, map_steps, start_weights, end_weights):
        local_m, local_w = alleles.shape
        targets, total_haps = start_weights.shape
        words = local_w * haps
        bits_word = total_haps // words
        reps = LANE * SUB // words
        vecs = bits_word // reps
        pack = LANE // local_w
        slots = pack * -(-local_m // pack)
        size = block_size(local_m)
        blocks = groups * (local_m // size)
        assert targets < SUB and targets <= groups and groups % 2 == 0 and slots % SUB == 0
        dims = (groups, haps, local_m, targets, words, bits_word)
        f32, i32 = jnp.float32, jnp.int32
        dma = pltpu.SemaphoreType.DMA
        tile = (SUB, LANE)
        out = pl.pallas_call(
            functools.partial(kernel, dims),
            out_shape=jax.ShapeDtypeStruct((targets, local_m), f32),
            in_specs=[pl.BlockSpec(memory_space=pltpu.HBM)] * 5,
            out_specs=pl.BlockSpec(memory_space=pltpu.VMEM),
            scratch_shapes=[
                pltpu.VMEM((local_m, local_w), i32),
                pltpu.VMEM((targets, local_m), i32),
                pltpu.SMEM((local_m,), i32),
                pltpu.VMEM((slots + SUB, LANE), i32),
                pltpu.VMEM((groups, 2 * SUB, LANE), i32),
                pltpu.VMEM((groups, haps * SUB, LANE), i32),
                pltpu.VMEM((groups * slots, *tile), i32),
                pltpu.VMEM((3, groups * slots + SUB, LANE), f32),
                pltpu.VMEM((2, targets, total_haps), f32),
                pltpu.VMEM((vecs * SUB * targets, LANE), f32),
                pltpu.VMEM((vecs, *tile), f32),
                pltpu.VMEM((vecs, *tile), f32),
                pltpu.VMEM((groups * slots, vecs, *tile), f32),
                pltpu.VMEM((blocks, size * (size + 1) // 2, *tile), f32),
                pltpu.VMEM((groups * slots, vecs, *tile), f32),
                pltpu.VMEM((blocks, vecs, *tile), f32),
                pltpu.VMEM((local_m, vecs, *tile), f32),
                pltpu.VMEM((groups * slots * SUB, LANE), f32),
                pltpu.VMEM((groups * slots * SUB, LANE), f32),
                pltpu.VMEM((groups, *tile), f32),
                pltpu.VMEM((targets, *tile), f32),
                dma((5,)), dma((groups, groups)), dma((groups,)), dma((groups, haps)), dma((groups, haps)),
                dma((groups,)), dma((targets,)),
            ],
            compiler_params=pltpu.CompilerParams(
                collective_id=0, has_side_effects=True, vmem_limit_bytes=60 * 1024 * 1024),
        )(alleles, observed.T, map_steps, start_weights, end_weights)
        return out.T

    in_specs = (P("grp", "hap"), P("grp", "hap"), P("grp"), P("hap", None), P("hap", None))
    return jax.shard_map(local, mesh=mesh, in_specs=in_specs, out_specs=P("grp", "hap"), check_vma=False)
```

time: 24 us -> 22.4 us (0.933)
  Pallas kernels: 22.3 us -> 20.9 us
    pallas_call x1, Pallas kernels: 22.3 us -> 20.9 us  [local(): pl.pallas_call(functools.partial(kernel, dims), out_shape=jax.ShapeDtypeS...]
    pallas_call x1 -> x0, local copies, waits for them, and re-layouts: 1.35 us -> none  [local(): pl.pallas_call(functools.partial(kernel, dims), out_shape=jax.ShapeDtypeS...]
    unnamed x0 -> x1, local copies, waits for them, and re-layouts: none -> 1.26 us
where the time goes in v1:
time: 22.4 us; the launch traced here: 22.2 us
  Pallas kernels  20.9 us (93%)
  local copies, waits for them, and re-layouts  1.26 us (6%)
    pallas_call x1, Pallas kernels, local(): pl.pallas_call(functools.partial(kernel, dims), out_shape=jax.ShapeDtypeS...  20.9 us
    unnamed x1, local copies, waits for them, and re-layouts  1.26 us

profile of v1, /device:TPU:0, one launch (start us, length us, event | category | flops | bytes accessed | tf_op | source)
XLA Modules:
  0.0 22.2 jit_solution(17606239214178529149)
XLA Ops:
  0.0 20.9 %shard_map.55 = f32[4,15]{1,0:T(4,128)} custom-call(s32[15,64]{1,0:T(8,128)} %alleles.1, s32[4,15]{1,0:T(4,128)} %bitcast.3, s32[15]{0:T(128)} %steps.1, f32[4,15360]{1,0:T(4,128)} %starts.1, f32[4,15360]{1,0:T(4,128)} %ends.1), custom_call_target="tpu_custom_call" | custom-call | tf_op jit(solution)/shard_map/pallas_call | solution.py:426
  20.9 1.3 %copy.7 = f32[15,4]{0,1:T(4,128)} copy(f32[15,4]{0,1:T(4,128)} %bitcast.2) | data formatting | bytes 480

commit v2 on v1

v2 whole, which is shorter than its diff:
```python
import functools
import jax
import jax.numpy as jnp
from jax import lax
from jax.experimental import pallas as pl
from jax.experimental.pallas import tpu as pltpu
from jax.sharding import PartitionSpec as P

error_rate = 0.01
map_unit = 100000.0
SUB, LANE = 8, 128
MESH = pl.DeviceIdType.MESH


def total(parts):
    parts = list(parts)
    while len(parts) > 1:
        parts = [a + b for a, b in zip(parts[::2], parts[1::2])] + parts[len(parts) // 2 * 2:]
    return parts[0]


def block_size(local_m):
    return next(n for n in (5, 4, 3, 2, 1) if local_m % n == 0)


def targets_each(targets, state_bytes):
    return 2 if targets % 2 == 0 and 4 * state_bytes <= 40 * 1024 * 1024 else 1


def kernel(dims, alleles, observed, steps, starts, ends, out,
           own_alleles, own_observed, own_steps, tmp, block, meta, recv, metas, bits, table, weights, staged,
           state_a, state_b, emit, runs, kept, kept_low, waiting, numer, denom, dos, out_recv,
           load_sem, send_sem, recv_sem, meta_send, meta_recv, out_send, out_recv_sem):
    groups, haps, local_m, targets, words, bits_word = dims
    total_haps = words * bits_word
    local_w = words // haps
    span = words // SUB
    reps = LANE // span
    vecs = bits_word // reps
    pack = LANE // local_w
    rows = -(-local_m // pack)
    slots = pack * rows
    share = haps // SUB
    size = block_size(local_m)
    blocks = local_m // size
    end_row = groups * slots
    each = targets_each(targets, groups * slots * total_haps * 4)
    teams = targets // each
    far = groups - 1
    g_me, h_me = lax.axis_index("grp"), lax.axis_index("hap")
    active = g_me < teams

    sources = [
        (alleles, own_alleles), (observed, own_observed), (steps, own_steps), (starts, weights.at[0]), (ends, weights.at[1])]
    loads = [pltpu.make_async_copy(source, target, load_sem.at[n]) for n, (source, target) in enumerate(sources)]
    for load in loads[:3]:
        load.start()

    def each_hap(act, first=0):
        if haps <= 8:
            for d in range(first, haps):
                act(lax.rem(h_me + d, haps))
        else:
            pl.loop(first, haps)(lambda d: act(lax.rem(h_me + d, haps)))

    def each_group(act):
        if groups <= 4:
            for g in reversed(range(groups)):
                act(g)
        else:
            pl.loop(0, groups)(lambda k: act(far - k))

    def not_me(g, h, act):
        pl.when((g != g_me) | (h != h_me))(act)

    barrier = pltpu.get_barrier_semaphore()

    def greet(g, h):
        pl.semaphore_signal(barrier, inc=1, device_id=(g, h), device_id_type=MESH)

    @pl.when(active)
    def _():
        each_group(lambda g: each_hap(lambda h: not_me(g, h, lambda: greet(g, h))))
        for load in loads[3:]:
            load.start()

    lane = lax.broadcasted_iota(jnp.int32, (SUB, LANE), 1)
    sub_at = lax.broadcasted_iota(jnp.int32, (SUB, LANE), 0)
    tmp[...] = jnp.zeros_like(tmp)
    for load in loads[:3]:
        load.wait()
    tmp[0:local_m, 0:local_w] = own_alleles[...]
    dense = tmp[0:SUB, :]
    for p in range(1, pack):
        dense = jnp.where(lane // local_w == p, pltpu.roll(tmp[p * rows:p * rows + SUB, :], p * local_w, 1), dense)
    block[...] = dense
    recv[g_me, pl.ds(pl.multiple_of(h_me * SUB, SUB), SUB), :] = dense
    tmp[0:targets, 0:local_m] = own_observed[...]
    columns = tmp[0:SUB, :]
    for i in range(local_m):
        columns = jnp.where((sub_at == targets) & (lane == i), own_steps[i], columns)
    meta[...] = columns
    metas[g_me] = columns

    def block_copy(g, h, from_g, from_h):
        return pltpu.make_async_remote_copy(
            src_ref=block, dst_ref=recv.at[from_g, pl.ds(pl.multiple_of(from_h * SUB, SUB), SUB), :],
            send_sem=send_sem.at[g, h], recv_sem=recv_sem.at[from_g, from_h],
            device_id=(g, h), device_id_type=MESH)

    def meta_copy(g, from_g):
        return pltpu.make_async_remote_copy(
            src_ref=meta, dst_ref=metas.at[from_g], send_sem=meta_send.at[g], recv_sem=meta_recv.at[from_g],
            device_id=(g, h_me), device_id_type=MESH)

    def each_send(act):
        for g in range(teams):
            pl.when(g != g_me)(lambda: act(meta_copy(g, g_me)))
            each_hap(lambda h: not_me(g, h, lambda: act(block_copy(g, h, g_me, h_me))))

    pl.semaphore_wait(barrier, teams * haps - jnp.where(active, 1, 0))
    each_send(lambda copy: copy.start())

    def add_up(value):
        for shift in (4, 2, 1):
            value = value + pltpu.roll(value, shift, 0)
        return jnp.broadcast_to(jnp.sum(value, axis=1, keepdims=True), (SUB, LANE))

    def arrange(which, state):
        for r in range(vecs):
            for s in range(SUB):
                at = s * vecs + r
                staged[at * targets:(at + 1) * targets, :] = weights[which, :, at * LANE:(at + 1) * LANE]
        first = g_me * each
        sums = [None] * each
        for q in range(vecs):
            spot = bits_word * (lane % span) + reps * q + lane // span
            chosen, within = spot // LANE, spot % LANE
            value = [jnp.zeros((SUB, LANE), jnp.float32)] * each
            for r in range(vecs):
                here = chosen == r
                for t in range(each):
                    source = staged[pl.ds(r * targets + first + t, SUB, stride=vecs * targets), :]
                    moved = jnp.take_along_axis(source, within, axis=1, mode="promise_in_bounds")
                    value[t] = jnp.where(here, moved, value[t])
            for t in range(each):
                state[t, q] = value[t]
                sums[t] = value[t] if q == 0 else sums[t] + value[t]
        return tuple(1.0 / add_up(sums[t]) for t in range(each))

    def read_meta(g):
        pl.when(g != g_me)(lambda: meta_copy(g_me, g).wait_recv())
        same = lax.broadcasted_iota(jnp.int32, (slots, LANE), 0) == lax.broadcasted_iota(jnp.int32, (slots, LANE), 1)

        def turned(at):
            values = jnp.broadcast_to(metas[g, pl.ds(at, 1), :].astype(jnp.float32), (slots, LANE))
            summed = jnp.sum(jnp.where(same, values, 0.0), axis=1, keepdims=True)
            return jnp.broadcast_to(summed, (slots, LANE))

        at = pl.ds(pl.multiple_of(g * slots, SUB), slots)
        for t in range(each):
            seen = turned(g_me * each + t)
            table[2 * t, at, :] = jnp.where(seen == 2.0, 1.0, jnp.where(seen == 1.0, 1.0 - error_rate, error_rate))
            table[2 * t + 1, at, :] = jnp.where(seen == 2.0, 1.0, jnp.where(seen == 0.0, 1.0 - error_rate, error_rate))
        rate = 1.0 - jnp.exp(-turned(targets) / map_unit)
        table[2 * each, at, :] = (rate / total_haps) / (1.0 - rate)

    def expand(g):
        each_hap(lambda h: not_me(g, h, lambda: block_copy(g_me, h_me, g, h).wait_recv()))
        for r in range(rows):
            parts = [recv[g, pl.ds(j * SUB + r, SUB, stride=SUB * share), :] for j in range(share)]
            for p in range(pack):
                n = p * rows + r
                if n >= local_m:
                    continue
                value = jnp.zeros((SUB, LANE), jnp.int32)
                for e in range(reps):
                    for j in range(share):
                        begin = e * span + j * local_w
                        shift = (begin - p * local_w) % LANE
                        piece = parts[j] if shift == 0 else pltpu.roll(parts[j], shift, 1)
                        piece = piece if e == 0 else jnp.right_shift(piece, e)
                        value = jnp.where((lane >= begin) & (lane < begin + local_w), piece, value)
                bits[g * slots + n] = value

    def row(kind, slot):
        return jnp.broadcast_to(table[kind, pl.ds(slot, 1), :], (SUB, LANE))

    def masked(words_in, q):
        return jnp.bitwise_and(words_in, 1 << (reps * q)) != 0

    pairs = [(j, i) for j in range(size) for i in range(j, size)]
    team = range(each)

    def prepare(g, n):
        at = g * slots + n * size
        sums = {}
        words_in = [bits[at + i] for i in range(size)]
        tops = [[(row(2 * t, at + i), row(2 * t + 1, at + i)) for i in range(size)] for t in team]
        for q in range(vecs):
            masks = [masked(words_in[i], q) for i in range(size)]
            for t in team:
                e = [jnp.where(masks[i], *tops[t][i]) for i in range(size)]
                for i in range(size):
                    emit[t, at + i, q] = e[i]
                for j in range(size):
                    run = e[j]
                    for i in range(j, size):
                        run = run if i == j else run * e[i]
                        sums[t, j, i] = run if q == 0 else sums[t, j, i] + run
        for t in team:
            for k, (j, i) in enumerate(pairs):
                runs[t, g * blocks + n, k] = add_up(sums[t, j, i])

    def solve(t, state, scale, g, n, order, after):
        at = g * slots + n * size
        sums = [None] * size
        for q in range(vecs):
            value = state[t, q]
            for i in order:
                value = value * emit[t, at + i, q]
                sums[i] = value if q == 0 else sums[i] + value
        span_of = {pair: runs[t, g * blocks + n, k] for k, pair in enumerate(pairs)}
        adds = {}
        last = None
        for i in order:
            slot = at + i
            if after:
                slot = slot + 1
                if i == size - 1:
                    ahead = jnp.where(g + 1 < groups, (g + 1) * slots, end_row)
                    slot = jnp.where(n * size + size == local_m, ahead, slot)
            adds[i] = row(2 * each, slot) if last is None else row(2 * each, slot) * last
            last = add_up(sums[i]) * scale
            for j in adds:
                last = last + adds[j] * span_of[min(i, j), max(i, j)]
        return adds, 1.0 / last

    up, down = list(range(size)), list(range(size))[::-1]

    def step_a(g, n, scale):
        at = g * slots + n * size
        solved = [solve(t, state_a, scale[t], g, n, up, False) for t in team]
        words_in = [bits[at + i] for i in range(size)]
        for q in range(vecs):
            masks = [masked(words_in[i], q) for i in range(size)]
            for t in team:
                value = state_a[t, q] * scale[t]
                for i in up:
                    value = emit[t, at + i, q] * (value + solved[t][0][i])
                    kept[t, at + i, q] = jnp.where(masks[i], value, 0.0)
                kept_low[t, g * blocks + n, q] = value
                state_a[t, q] = value
        return tuple(solved[t][1] for t in team)

    def put_sums(t, g, n, tops, low):
        for i in range(size):
            at = pl.ds(pl.multiple_of((g * slots + n * size + i) * SUB, SUB), SUB)
            numer[t, at, :] = tops[i]
            denom[t, at, :] = low

    def step_b(g, n, scale, score):
        at = g * slots + n * size
        result = []
        for t in team:
            adds, after = solve(t, state_b, scale[t], g, n, down, True)
            result.append(after)
            tops, low = [None] * size, None
            for q in range(vecs):
                value = state_b[t, q] * scale[t]
                for i in down:
                    value = value + adds[i]
                    if score:
                        part = kept[t, at + i, q] * value
                        tops[i] = part if q == 0 else tops[i] + part
                        if i == size - 1:
                            part = kept_low[t, g * blocks + n, q] * value
                            low = part if q == 0 else low + part
                    else:
                        waiting[t, n * size + i, q] = value
                    value = emit[t, at + i, q] * value
                state_b[t, q] = value
            if score:
                put_sums(t, g, n, tops, low)
        return tuple(result)

    def score_waiting(g, n):
        at = g * slots + n * size
        end = n * size + size - 1
        for t in team:
            tops = [total(kept[t, at + i, q] * waiting[t, n * size + i, q] for q in range(vecs)) for i in range(size)]
            put_sums(t, g, n, tops, total(kept_low[t, g * blocks + n, q] * waiting[t, end, q] for q in range(vecs)))

    def out_copy(g, from_g):
        return pltpu.make_async_remote_copy(
            src_ref=dos.at[g], dst_ref=out_recv.at[from_g], send_sem=out_send.at[g],
            recv_sem=out_recv_sem.at[from_g], device_id=(g, h_me), device_id_type=MESH)

    row_at = lax.broadcasted_iota(jnp.int32, (slots, LANE), 0)
    own_lane = (lax.broadcasted_iota(jnp.int32, (slots, LANE), 1) == row_at) & (row_at < local_m)

    def finish(g):
        result = jnp.zeros((SUB, LANE), jnp.float32)
        for t in team:
            def gathered(sums):
                parts = [sums[t, pl.ds(g * slots * SUB + k, slots, stride=SUB), :] for k in range(SUB)]
                return jnp.sum(total(parts), axis=1, keepdims=True)

            value = jnp.broadcast_to(gathered(numer) / gathered(denom), (slots, LANE))
            value = jnp.sum(jnp.where(own_lane, value, 0.0), axis=0, keepdims=True)
            result = jnp.where(sub_at == g_me * each + t, jnp.broadcast_to(value, (SUB, LANE)), result)
        dos[g] = result
        pl.when(g != g_me)(lambda: out_copy(g, g_me).start())

    @pl.when(active)
    def _():
        for load in loads[3:]:
            load.wait()
        scale_a = arrange(0, state_a)
        scale_b = arrange(1, state_b)
        table[2 * each, end_row:end_row + SUB, :] = jnp.zeros((SUB, LANE), jnp.float32)

        def first_pass(g, scale):
            read_meta(g)
            expand(g)
            for n in range(blocks):
                prepare(g, n)
                scale = step_a(g, n, scale)
            return scale

        scale_a = lax.fori_loop(0, far, first_pass, scale_a)
        read_meta(far)
        expand(far)
        ready = set()
        for n in range(blocks):
            for k in (n, blocks - 1 - n):
                if k not in ready:
                    ready.add(k)
                    prepare(far, k)
            scale_a = step_a(far, n, scale_a)
            scale_b = step_b(far, blocks - 1 - n, scale_b, False)
        for n in range(blocks):
            score_waiting(far, n)

        def second_pass(k, scale):
            g = far - 1 - k
            finish(g + 1)
            for n in reversed(range(blocks)):
                scale = step_b(g, n, scale, True)
            return scale

        lax.fori_loop(0, far, second_pass, scale_b)
        finish(0)
        out_recv[g_me] = dos[g_me]

    each_send(lambda copy: copy.wait_send())
    for g in range(teams):
        pl.when(g != g_me)(lambda: out_copy(g_me, g).wait_recv())
    result = out_recv[0]
    for g in range(1, teams):
        result = jnp.where(sub_at // each == g, out_recv[g], result)
    out[...] = result[0:targets, 0:local_m]

    @pl.when(active)
    def _():
        each_group(lambda g: pl.when(g != g_me)(lambda: out_copy(g, g_me).wait_send()))


def solution(mesh):
    groups, haps = mesh.shape["grp"], mesh.shape["hap"]

    def local(alleles, observed, map_steps, start_weights, end_weights):
        local_m, local_w = alleles.shape
        targets, total_haps = start_weights.shape
        words = local_w * haps
        bits_word = total_haps // words
        reps = LANE * SUB // words
        vecs = bits_word // reps
        pack = LANE // local_w
        slots = pack * -(-local_m // pack)
        size = block_size(local_m)
        blocks = groups * (local_m // size)
        each = targets_each(targets, groups * slots * total_haps * 4)
        teams = targets // each
        assert targets < SUB and teams <= groups and slots % SUB == 0
        dims = (groups, haps, local_m, targets, words, bits_word)
        f32, i32 = jnp.float32, jnp.int32
        dma = pltpu.SemaphoreType.DMA
        tile = (SUB, LANE)
        out = pl.pallas_call(
            functools.partial(kernel, dims),
            out_shape=pltpu.VMEM((targets, local_m), f32),
            in_specs=[pl.BlockSpec(memory_space=pltpu.HBM)] * 5,
            out_specs=pl.BlockSpec(memory_space=pltpu.VMEM),
            scratch_shapes=[
                pltpu.VMEM((local_m, local_w), i32),
                pltpu.VMEM((targets, local_m), i32),
                pltpu.SMEM((local_m,), i32),
                pltpu.VMEM((slots + SUB, LANE), i32),
                pltpu.VMEM(tile, i32),
                pltpu.VMEM(tile, i32),
                pltpu.VMEM((groups, haps * SUB, LANE), i32),
                pltpu.VMEM((groups, *tile), i32),
                pltpu.VMEM((groups * slots, *tile), i32),
                pltpu.VMEM((2 * each + 1, groups * slots + SUB, LANE), f32),
                pltpu.VMEM((2, targets, total_haps), f32),
                pltpu.VMEM((vecs * SUB * targets, LANE), f32),
                pltpu.VMEM((each, vecs, *tile), f32),
                pltpu.VMEM((each, vecs, *tile), f32),
                pltpu.VMEM((each, groups * slots, vecs, *tile), f32),
                pltpu.VMEM((each, blocks, size * (size + 1) // 2, *tile), f32),
                pltpu.VMEM((each, groups * slots, vecs, *tile), f32),
                pltpu.VMEM((each, blocks, vecs, *tile), f32),
                pltpu.VMEM((each, local_m, vecs, *tile), f32),
                pltpu.VMEM((each, groups * slots * SUB, LANE), f32),
                pltpu.VMEM((each, groups * slots * SUB, LANE), f32),
                pltpu.VMEM((groups, *tile), f32),
                pltpu.VMEM((teams, *tile), f32),
                dma((5,)), dma((teams, haps)), dma((groups, haps)), dma((teams,)), dma((groups,)),
                dma((groups,)), dma((teams,)),
            ],
            compiler_params=pltpu.CompilerParams(
                collective_id=0, has_side_effects=True, vmem_limit_bytes=60 * 1024 * 1024),
        )(alleles, observed.T, map_steps, start_weights, end_weights)
        return out.T

    in_specs = (P("grp", "hap"), P("grp", "hap"), P("grp"), P("hap", None), P("hap", None))
    return jax.shard_map(local, mesh=mesh, in_specs=in_specs, out_specs=P("grp", "hap"), check_vma=False)
```

time: 22.4 us -> 19.5 us (0.87)
  Pallas kernels: 20.9 us -> 18.7 us
  local copies, waits for them, and re-layouts: 1.26 us -> 0.58 us
    pallas_call x1, Pallas kernels: 20.9 us -> 18.7 us  [local(): pl.pallas_call(functools.partial(kernel, dims), out_shape=pltpu.VMEM((tar...]
    unnamed x1, local copies, waits for them, and re-layouts: 1.26 us -> 0.58 us
where the time goes in v2:
time: 19.5 us; the launch traced here: 19.3 us
  Pallas kernels  18.7 us (96%)
  local copies, waits for them, and re-layouts  0.58 us (3%)
    pallas_call x1, Pallas kernels, local(): pl.pallas_call(functools.partial(kernel, dims), out_shape=pltpu.VMEM((tar...  18.7 us
    unnamed x1, local copies, waits for them, and re-layouts  0.58 us

profile of v2, /device:TPU:0, one launch (start us, length us, event | category | flops | bytes accessed | tf_op | source)
XLA Modules:
  0.0 19.3 jit_solution(5882933276940541059)
XLA Ops:
  0.0 18.7 %shard_map.55 = f32[4,15]{1,0:T(4,128)S(1)} custom-call(s32[15,64]{1,0:T(8,128)} %alleles.1, s32[4,15]{1,0:T(4,128)} %bitcast.3, s32[15]{0:T(128)} %steps.1, f32[4,15360]{1,0:T(4,128)} %starts.1, f32[4,15360]{1,0:T(4,128)} %ends.1), custom_call_target="tpu_custom_call" | custom-call | tf_op jit(solution)/shard_map/pallas_call | solution.py:390
  18.7 0.6 %copy.7 = f32[15,4]{0,1:T(4,128)} copy(f32[15,4]{0,1:T(4,128)S(1)} %bitcast.2) | data formatting | bytes 480

commit v3 on v2

--- a/solution.py
+++ b/solution.py
@@ -194,25 +194,58 @@
 
     def prepare(g, n):
         at = g * slots + n * size
-        sums = {}
         words_in = [bits[at + i] for i in range(size)]
-        tops = [[(row(2 * t, at + i), row(2 * t + 1, at + i)) for i in range(size)] for t in team]
-        for q in range(vecs):
-            masks = [masked(words_in[i], q) for i in range(size)]
-            for t in team:
-                e = [jnp.where(masks[i], *tops[t][i]) for i in range(size)]
+        for t in team:
+            tops = [(row(2 * t, at + i), row(2 * t + 1, at + i)) for i in range(size)]
+            for q in range(vecs):
                 for i in range(size):
-                    emit[t, at + i, q] = e[i]
-                for j in range(size):
-                    run = e[j]
-                    for i in range(j, size):
-                        run = run if i == j else run * e[i]
-                        sums[t, j, i] = run if q == 0 else sums[t, j, i] + run
+                    emit[t, at + i, q] = jnp.where(masked(words_in[i], q), *tops[i])
+
+    inner = min(size, 4)
+    used = sum(1 << (reps * q) for q in range(vecs))
+
+    def count_patterns(g):
+        counts = [jnp.zeros((SUB, LANE), jnp.float32)] * (1 << (size - inner))
+        for n in range(blocks):
+            sets = [jnp.full((SUB, LANE), used, jnp.int32)]
+            for i in range(size):
+                word = bits[g * slots + n * size + i]
+                other = jnp.bitwise_not(word)
+                sets = [jnp.bitwise_and(x, other) for x in sets] + [jnp.bitwise_and(x, word) for x in sets]
+            sets += [jnp.zeros((SUB, LANE), jnp.int32)] * (LANE // SUB - len(sets))
+            held = jnp.concatenate([lax.population_count(x).astype(jnp.float32) for x in sets], axis=0)
+            found = lax.dot_general(
+                jnp.ones((SUB, LANE), jnp.bfloat16), held.astype(jnp.bfloat16), (((1,), (1,)), ((), ())),
+                preferred_element_type=jnp.float32)
+            counts = [jnp.where(sub_at == n, found[:, k * LANE:(k + 1) * LANE], c) for k, c in enumerate(counts)]
+        return counts
+
+    def make_spans(g):
+        counts = count_patterns(g)
+        pattern = lane // SUB
         for t in team:
-            for k, (j, i) in enumerate(pairs):
-                runs[t, g * blocks + n, k] = add_up(sums[t, j, i])
-
-    def solve(t, state, scale, g, n, order, after):
+            def rows_of(kind, i):
+                return table[kind, pl.ds(g * slots + i, SUB, stride=size), :]
+
+            e = [
+                jnp.where(jnp.bitwise_and(jnp.right_shift(pattern, i), 1) != 0, rows_of(2 * t, i), rows_of(2 * t + 1, i))
+                for i in range(inner)
+            ]
+            whole = total(counts)
+            if size > inner:
+                last = counts[0] * rows_of(2 * t + 1, inner) + counts[1] * rows_of(2 * t, inner)
+            for j in range(size):
+                run = None
+                for i in range(j, size):
+                    if i < inner:
+                        run = e[i] if run is None else run * e[i]
+                        value = whole * run
+                    else:
+                        value = last if run is None else last * run
+                    summed = jnp.broadcast_to(jnp.sum(value, axis=1, keepdims=True), (SUB, LANE))
+                    runs[t, g, pairs.index((j, i))] = summed
+
+    def ahead(t, state, g, n, order):
         at = g * slots + n * size
         sums = [None] * size
         for q in range(vecs):
@@ -220,7 +253,12 @@
             for i in order:
                 value = value * emit[t, at + i, q]
                 sums[i] = value if q == 0 else sums[i] + value
-        span_of = {pair: runs[t, g * blocks + n, k] for k, pair in enumerate(pairs)}
+        return [add_up(value) for value in sums]
+
+    def solve(t, sums, scale, g, n, order, after):
+        at = g * slots + n * size
+        span_of = {
+            pair: jnp.broadcast_to(runs[t, g, k, pl.ds(n, 1), :], (SUB, LANE)) for k, pair in enumerate(pairs)}
         adds = {}
         last = None
         for i in order:
@@ -231,7 +269,7 @@
                     ahead = jnp.where(g + 1 < groups, (g + 1) * slots, end_row)
                     slot = jnp.where(n * size + size == local_m, ahead, slot)
             adds[i] = row(2 * each, slot) if last is None else row(2 * each, slot) * last
-            last = add_up(sums[i]) * scale
+            last = sums[i] * scale
             for j in adds:
                 last = last + adds[j] * span_of[min(i, j), max(i, j)]
         return adds, 1.0 / last
@@ -240,7 +278,8 @@
 
     def step_a(g, n, scale):
         at = g * slots + n * size
-        solved = [solve(t, state_a, scale[t], g, n, up, False) for t in team]
+        sums = [ahead(t, state_a, g, n, up) for t in team]
+        solved = [solve(t, sums[t], scale[t], g, n, up, False) for t in team]
         words_in = [bits[at + i] for i in range(size)]
         for q in range(vecs):
             masks = [masked(words_in[i], q) for i in range(size)]
@@ -259,37 +298,34 @@
             numer[t, at, :] = tops[i]
             denom[t, at, :] = low
 
-    def step_b(g, n, scale, score):
-        at = g * slots + n * size
-        result = []
+    def step_b(g, n, scale, earlier):
+        at = g * slots + n * size
+        sums = [ahead(t, state_b, g, n, down) for t in team]
+        if earlier is not None:
+            score_waiting(*earlier)
+        solved = [solve(t, sums[t], scale[t], g, n, down, True) for t in team]
         for t in team:
-            adds, after = solve(t, state_b, scale[t], g, n, down, True)
-            result.append(after)
-            tops, low = [None] * size, None
             for q in range(vecs):
                 value = state_b[t, q] * scale[t]
                 for i in down:
-                    value = value + adds[i]
-                    if score:
-                        part = kept[t, at + i, q] * value
-                        tops[i] = part if q == 0 else tops[i] + part
-                        if i == size - 1:
-                            part = kept_low[t, g * blocks + n, q] * value
-                            low = part if q == 0 else low + part
-                    else:
-                        waiting[t, n * size + i, q] = value
+                    value = value + solved[t][0][i]
+                    waiting[t, n * size + i, q] = value
                     value = emit[t, at + i, q] * value
                 state_b[t, q] = value
-            if score:
-                put_sums(t, g, n, tops, low)
-        return tuple(result)
+        return tuple(solved[t][1] for t in team)
 
     def score_waiting(g, n):
         at = g * slots + n * size
         end = n * size + size - 1
         for t in team:
-            tops = [total(kept[t, at + i, q] * waiting[t, n * size + i, q] for q in range(vecs)) for i in range(size)]
-            put_sums(t, g, n, tops, total(kept_low[t, g * blocks + n, q] * waiting[t, end, q] for q in range(vecs)))
+            tops, low = [None] * size, None
+            for q in range(vecs):
+                for i in range(size):
+                    part = kept[t, at + i, q] * waiting[t, n * size + i, q]
+                    tops[i] = part if q == 0 else tops[i] + part
+                part = kept_low[t, g * blocks + n, q] * waiting[t, end, q]
+                low = part if q == 0 else low + part
+            put_sums(t, g, n, tops, low)
 
     def out_copy(g, from_g):
         return pltpu.make_async_remote_copy(
@@ -323,6 +359,7 @@
         def first_pass(g, scale):
             read_meta(g)
             expand(g)
+            make_spans(g)
             for n in range(blocks):
                 prepare(g, n)
                 scale = step_a(g, n, scale)
@@ -331,6 +368,7 @@
         scale_a = lax.fori_loop(0, far, first_pass, scale_a)
         read_meta(far)
         expand(far)
+        make_spans(far)
         ready = set()
         for n in range(blocks):
             for k in (n, blocks - 1 - n):
@@ -338,18 +376,20 @@
                     ready.add(k)
                     prepare(far, k)
             scale_a = step_a(far, n, scale_a)
-            scale_b = step_b(far, blocks - 1 - n, scale_b, False)
-        for n in range(blocks):
+            scale_b = step_b(far, blocks - 1 - n, scale_b, None)
+        for n in range(1, blocks):
             score_waiting(far, n)
 
         def second_pass(k, scale):
             g = far - 1 - k
-            finish(g + 1)
             for n in reversed(range(blocks)):
-                scale = step_b(g, n, scale, True)
+                scale = step_b(g, n, scale, (g, n + 1) if n + 1 < blocks else (g + 1, 0))
+                if n + 1 == blocks:
+                    finish(g + 1)
             return scale
 
         lax.fori_loop(0, far, second_pass, scale_b)
+        score_waiting(0, 0)
         finish(0)
         out_recv[g_me] = dos[g_me]
 
@@ -402,13 +442,13 @@
                 pltpu.VMEM((groups, haps * SUB, LANE), i32),
                 pltpu.VMEM((groups, *tile), i32),
                 pltpu.VMEM((groups * slots, *tile), i32),
-                pltpu.VMEM((2 * each + 1, groups * slots + SUB, LANE), f32),
+                pltpu.VMEM((2 * each + 1, groups * slots + (size + 1) * SUB, LANE), f32),
                 pltpu.VMEM((2, targets, total_haps), f32),
                 pltpu.VMEM((vecs * SUB * targets, LANE), f32),
                 pltpu.VMEM((each, vecs, *tile), f32),
                 pltpu.VMEM((each, vecs, *tile), f32),
                 pltpu.VMEM((each, groups * slots, vecs, *tile), f32),
-                pltpu.VMEM((each, blocks, size * (size + 1) // 2, *tile), f32),
+                pltpu.VMEM((each, groups, size * (size + 1) // 2, *tile), f32),
                 pltpu.VMEM((each, groups * slots, vecs, *tile), f32),
                 pltpu.VMEM((each, blocks, vecs, *tile), f32),
                 pltpu.VMEM((each, local_m, vecs, *tile), f32),

time: 19.5 us -> 18.6 us (0.954)
  Pallas kernels: 18.7 us -> 17.9 us
    pallas_call x1, Pallas kernels: 18.7 us -> 17.9 us  [local(): pl.pallas_call(functools.partial(kernel, dims), out_shape=pltpu.VMEM((tar...]
where the time goes in v3:
time: 18.6 us; the launch traced here: 18.5 us
  Pallas kernels  17.9 us (96%)
  local copies, waits for them, and re-layouts  0.58 us (3%)
    pallas_call x1, Pallas kernels, local(): pl.pallas_call(functools.partial(kernel, dims), out_shape=pltpu.VMEM((tar...  17.9 us
    unnamed x1, local copies, waits for them, and re-layouts  0.58 us

profile of v3, /device:TPU:0, one launch (start us, length us, event | category | flops | bytes accessed | tf_op | source)
XLA Modules:
  0.0 18.5 jit_solution(13628611236206085759)
XLA Ops:
  0.0 17.9 %shard_map.55 = f32[4,15]{1,0:T(4,128)S(1)} custom-call(s32[15,64]{1,0:T(8,128)} %alleles.1, s32[4,15]{1,0:T(4,128)} %bitcast.3, s32[15]{0:T(128)} %steps.1, f32[4,15360]{1,0:T(4,128)} %starts.1, f32[4,15360]{1,0:T(4,128)} %ends.1), custom_call_target="tpu_custom_call" | custom-call | tf_op jit(solution)/shard_map/pallas_call | solution.py:430
  17.9 0.6 %copy.7 = f32[15,4]{0,1:T(4,128)} copy(f32[15,4]{0,1:T(4,128)S(1)} %bitcast.2) | data formatting | bytes 480

commit v4 on v2

v4 whole, which is shorter than its diff:
```python
import functools
import jax
import jax.numpy as jnp
from jax import lax
from jax.experimental import pallas as pl
from jax.experimental.pallas import tpu as pltpu
from jax.sharding import PartitionSpec as P

error_rate = 0.01
map_unit = 100000.0
SUB, LANE = 8, 128
MESH = pl.DeviceIdType.MESH


def total(parts):
    parts = list(parts)
    while len(parts) > 1:
        parts = [a + b for a, b in zip(parts[::2], parts[1::2])] + parts[len(parts) // 2 * 2:]
    return parts[0]


def block_size(local_m):
    return next(n for n in (5, 4, 3, 2, 1) if local_m % n == 0)


def split_targets(targets, state_bytes):
    if targets > 1 and 2 * (targets - 1) * state_bytes <= 40 * 1024 * 1024:
        return targets // 2, targets - targets // 2
    return (1,) * targets


def kernel(dims, alleles, observed, steps, starts, ends, out,
           own_alleles, own_observed, own_steps, tmp, block, meta, recv, metas, bits, table, weights, staged,
           state_a, state_b, emit, runs, kept, kept_low, waiting, numer, denom, dos, out_recv,
           load_sem, send_sem, recv_sem, meta_send, meta_recv, out_send, out_recv_sem):
    groups, haps, local_m, targets, words, bits_word = dims
    total_haps = words * bits_word
    local_w = words // haps
    span = words // SUB
    reps = LANE // span
    vecs = bits_word // reps
    pack = LANE // local_w
    rows = -(-local_m // pack)
    slots = pack * rows
    share = haps // SUB
    size = block_size(local_m)
    blocks = local_m // size
    end_row = groups * slots
    split = split_targets(targets, groups * slots * total_haps * 4)
    teams = len(split)
    far = groups - 1
    g_me, h_me = lax.axis_index("grp"), lax.axis_index("hap")
    active = g_me < teams

    sources = [
        (alleles, own_alleles), (observed, own_observed), (steps, own_steps), (starts, weights.at[0]), (ends, weights.at[1])]
    loads = [pltpu.make_async_copy(source, target, load_sem.at[n]) for n, (source, target) in enumerate(sources)]
    for load in loads[:3]:
        load.start()

    def each_hap(act, first=0):
        if haps <= 8:
            for d in range(first, haps):
                act(lax.rem(h_me + d, haps))
        else:
            pl.loop(first, haps)(lambda d: act(lax.rem(h_me + d, haps)))

    def each_group(act):
        if groups <= 4:
            for g in reversed(range(groups)):
                act(g)
        else:
            pl.loop(0, groups)(lambda k: act(far - k))

    def not_me(g, h, act):
        pl.when((g != g_me) | (h != h_me))(act)

    barrier = pltpu.get_barrier_semaphore()

    def greet(g, h):
        pl.semaphore_signal(barrier, inc=1, device_id=(g, h), device_id_type=MESH)

    @pl.when(active)
    def _():
        each_group(lambda g: each_hap(lambda h: not_me(g, h, lambda: greet(g, h))))
        for load in loads[3:]:
            load.start()

    lane = lax.broadcasted_iota(jnp.int32, (SUB, LANE), 1)
    sub_at = lax.broadcasted_iota(jnp.int32, (SUB, LANE), 0)
    tmp[...] = jnp.zeros_like(tmp)
    for load in loads[:3]:
        load.wait()
    tmp[0:local_m, 0:local_w] = own_alleles[...]
    dense = tmp[0:SUB, :]
    for p in range(1, pack):
        dense = jnp.where(lane // local_w == p, pltpu.roll(tmp[p * rows:p * rows + SUB, :], p * local_w, 1), dense)
    block[...] = dense
    recv[g_me, pl.ds(pl.multiple_of(h_me * SUB, SUB), SUB), :] = dense
    tmp[0:targets, 0:local_m] = own_observed[...]
    columns = tmp[0:SUB, :]
    for i in range(local_m):
        columns = jnp.where((sub_at == targets) & (lane == i), own_steps[i], columns)
    meta[...] = columns
    metas[g_me] = columns

    def block_copy(g, h, from_g, from_h):
        return pltpu.make_async_remote_copy(
            src_ref=block, dst_ref=recv.at[from_g, pl.ds(pl.multiple_of(from_h * SUB, SUB), SUB), :],
            send_sem=send_sem.at[g, h], recv_sem=recv_sem.at[from_g, from_h],
            device_id=(g, h), device_id_type=MESH)

    def meta_copy(g, from_g):
        return pltpu.make_async_remote_copy(
            src_ref=meta, dst_ref=metas.at[from_g], send_sem=meta_send.at[g], recv_sem=meta_recv.at[from_g],
            device_id=(g, h_me), device_id_type=MESH)

    def each_send(act):
        for g in reversed(range(teams)):
            pl.when(g != g_me)(lambda: act(meta_copy(g, g_me)))
            each_hap(lambda h: not_me(g, h, lambda: act(block_copy(g, h, g_me, h_me))))

    pl.semaphore_wait(barrier, teams * haps - jnp.where(active, 1, 0))
    each_send(lambda copy: copy.start())

    def out_copy(g, from_g):
        return pltpu.make_async_remote_copy(
            src_ref=dos.at[g], dst_ref=out_recv.at[from_g], send_sem=out_send.at[g],
            recv_sem=out_recv_sem.at[from_g], device_id=(g, h_me), device_id_type=MESH)

    def run(first, each):
        def add_up(value):
            for shift in (4, 2, 1):
                value = value + pltpu.roll(value, shift, 0)
            return jnp.broadcast_to(jnp.sum(value, axis=1, keepdims=True), (SUB, LANE))

        def arrange(which, state):
            for r in range(vecs):
                for s in range(SUB):
                    at = s * vecs + r
                    staged[at * targets:(at + 1) * targets, :] = weights[which, :, at * LANE:(at + 1) * LANE]
            sums = [None] * each
            for q in range(vecs):
                spot = bits_word * (lane % span) + reps * q + lane // span
                chosen, within = spot // LANE, spot % LANE
                value = [jnp.zeros((SUB, LANE), jnp.float32)] * each
                for r in range(vecs):
                    here = chosen == r
                    for t in range(each):
                        source = staged[pl.ds(r * targets + first + t, SUB, stride=vecs * targets), :]
                        moved = jnp.take_along_axis(source, within, axis=1, mode="promise_in_bounds")
                        value[t] = jnp.where(here, moved, value[t])
                for t in range(each):
                    state[t, q] = value[t]
                    sums[t] = value[t] if q == 0 else sums[t] + value[t]
            return tuple(1.0 / add_up(sums[t]) for t in range(each))

        def arrived(g):
            pl.when(g != g_me)(lambda: meta_copy(g_me, g).wait_recv())
            each_hap(lambda h: not_me(g, h, lambda: block_copy(g_me, h_me, g, h).wait_recv()))

        def read_meta(g):
            same = lax.broadcasted_iota(jnp.int32, (slots, LANE), 0) == lax.broadcasted_iota(jnp.int32, (slots, LANE), 1)

            def turned(at):
                values = jnp.broadcast_to(metas[g, pl.ds(at, 1), :].astype(jnp.float32), (slots, LANE))
                summed = jnp.sum(jnp.where(same, values, 0.0), axis=1, keepdims=True)
                return jnp.broadcast_to(summed, (slots, LANE))

            at = pl.ds(pl.multiple_of(g * slots, SUB), slots)
            for t in range(each):
                seen = turned(first + t)
                table[2 * t, at, :] = jnp.where(seen == 2.0, 1.0, jnp.where(seen == 1.0, 1.0 - error_rate, error_rate))
                table[2 * t + 1, at, :] = jnp.where(seen == 2.0, 1.0, jnp.where(seen == 0.0, 1.0 - error_rate, error_rate))
            rate = 1.0 - jnp.exp(-turned(targets) / map_unit)
            table[2 * each, at, :] = (rate / total_haps) / (1.0 - rate)

        def expand(g):
            for r in range(rows):
                parts = [recv[g, pl.ds(j * SUB + r, SUB, stride=SUB * share), :] for j in range(share)]
                for p in range(pack):
                    n = p * rows + r
                    if n >= local_m:
                        continue
                    value = jnp.zeros((SUB, LANE), jnp.int32)
                    for e in range(reps):
                        for j in range(share):
                            begin = e * span + j * local_w
                            shift = (begin - p * local_w) % LANE
                            piece = parts[j] if shift == 0 else pltpu.roll(parts[j], shift, 1)
                            piece = piece if e == 0 else jnp.right_shift(piece, e)
                            value = jnp.where((lane >= begin) & (lane < begin + local_w), piece, value)
                    bits[g * slots + n] = value

        def row(kind, slot):
            return jnp.broadcast_to(table[kind, pl.ds(slot, 1), :], (SUB, LANE))

        def masked(words_in, q):
            return jnp.bitwise_and(words_in, 1 << (reps * q)) != 0

        pairs = [(j, i) for j in range(size) for i in range(j, size)]
        team = range(each)

        def prepare(g, n):
            at = g * slots + n * size
            words_in = [bits[at + i] for i in range(size)]
            for t in team:
                tops = [(row(2 * t, at + i), row(2 * t + 1, at + i)) for i in range(size)]
                for q in range(vecs):
                    for i in range(size):
                        mask = masked(words_in[i], q)
                        emit[t, at + i, q] = jnp.where(mask, *tops[i])
                        kept[t, at + i, q] = jnp.where(mask, tops[i][0], 0.0)

        inner = min(size, 4)
        used = sum(1 << (reps * q) for q in range(vecs))

        def count_patterns(g):
            counts = [jnp.zeros((SUB, LANE), jnp.float32)] * (1 << (size - inner))
            for n in range(blocks):
                sets = [jnp.full((SUB, LANE), used, jnp.int32)]
                for i in range(size):
                    word = bits[g * slots + n * size + i]
                    other = jnp.bitwise_not(word)
                    sets = [jnp.bitwise_and(x, other) for x in sets] + [jnp.bitwise_and(x, word) for x in sets]
                sets += [jnp.zeros((SUB, LANE), jnp.int32)] * (LANE // SUB - len(sets))
                held = jnp.concatenate([lax.population_count(x).astype(jnp.float32) for x in sets], axis=0)
                found = lax.dot_general(
                    jnp.ones((SUB, LANE), jnp.bfloat16), held.astype(jnp.bfloat16), (((1,), (1,)), ((), ())),
                    preferred_element_type=jnp.float32)
                counts = [jnp.where(sub_at == n, found[:, k * LANE:(k + 1) * LANE], c) for k, c in enumerate(counts)]
            return counts

        def make_spans(g):
            counts = count_patterns(g)
            pattern = lane // SUB
            for t in team:
                def rows_of(kind, i):
                    return table[kind, pl.ds(g * slots + i, SUB, stride=size), :]

                e = [
                    jnp.where(jnp.bitwise_and(jnp.right_shift(pattern, i), 1) != 0, rows_of(2 * t, i), rows_of(2 * t + 1, i))
                    for i in range(inner)
                ]
                whole = total(counts)
                if size > inner:
                    last = counts[0] * rows_of(2 * t + 1, inner) + counts[1] * rows_of(2 * t, inner)
                for j in range(size):
                    run = None
                    for i in range(j, size):
                        if i < inner:
                            run = e[i] if run is None else run * e[i]
                            value = whole * run
                        else:
                            value = last if run is None else last * run
                        summed = jnp.broadcast_to(jnp.sum(value, axis=1, keepdims=True), (SUB, LANE))
                        runs[t, g, pairs.index((j, i))] = summed

        def ahead(t, state, g, n, order):
            at = g * slots + n * size
            sums = [None] * size
            for q in range(vecs):
                value = state[t, q]
                for i in order:
                    value = value * emit[t, at + i, q]
                    sums[i] = value if q == 0 else sums[i] + value
            return [add_up(value) for value in sums]

        def solve(t, sums, scale, g, n, order, after):
            at = g * slots + n * size
            span_of = {
                pair: jnp.broadcast_to(runs[t, g, k, pl.ds(n, 1), :], (SUB, LANE)) for k, pair in enumerate(pairs)}
            adds = {}
            last = None
            for i in order:
                slot = at + i
                if after:
                    slot = slot + 1
                    if i == size - 1:
                        ahead = jnp.where(g + 1 < groups, (g + 1) * slots, end_row)
                        slot = jnp.where(n * size + size == local_m, ahead, slot)
                adds[i] = row(2 * each, slot) if last is None else row(2 * each, slot) * last
                last = sums[i] * scale
                for j in adds:
                    last = last + adds[j] * span_of[min(i, j), max(i, j)]
            return adds, 1.0 / last

        up, down = list(range(size)), list(range(size))[::-1]

        def prepare_ahead(g, n):
            at = g * slots + n * size
            words_in = [bits[at + i] for i in range(size)]
            sums = [[None] * size for t in team]
            tops = [[(row(2 * t, at + i), row(2 * t + 1, at + i)) for i in range(size)] for t in team]
            for q in range(vecs):
                masks = [masked(words_in[i], q) for i in range(size)]
                for t in team:
                    value = state_a[t, q]
                    for i in up:
                        e = jnp.where(masks[i], *tops[t][i])
                        emit[t, at + i, q] = e
                        kept[t, at + i, q] = jnp.where(masks[i], tops[t][i][0], 0.0)
                        value = value * e
                        sums[t][i] = value if q == 0 else sums[t][i] + value
            return [[add_up(value) for value in sums[t]] for t in team]

        def step_a(g, n, scale, fresh):
            at = g * slots + n * size
            sums = prepare_ahead(g, n) if fresh else [ahead(t, state_a, g, n, up) for t in team]
            solved = [solve(t, sums[t], scale[t], g, n, up, False) for t in team]
            for t in team:
                for q in range(vecs):
                    value = state_a[t, q] * scale[t]
                    for i in up:
                        moved = value + solved[t][0][i]
                        kept[t, at + i, q] = kept[t, at + i, q] * moved
                        value = emit[t, at + i, q] * moved
                    kept_low[t, g * blocks + n, q] = value
                    state_a[t, q] = value
            return tuple(solved[t][1] for t in team)

        def put_sums(t, g, n, tops, low):
            for i in range(size):
                at = pl.ds(pl.multiple_of((g * slots + n * size + i) * SUB, SUB), SUB)
                numer[t, at, :] = tops[i]
                denom[t, at, :] = low

        def step_b(t, g, n, scale, sums, score):
            at = g * slots + n * size
            adds, after = solve(t, sums, scale, g, n, down, True)
            tops, low = [None] * size, None
            for q in range(vecs):
                value = state_b[t, q] * scale
                for i in down:
                    value = value + adds[i]
                    if not score:
                        waiting[t, n * size + i, q] = value
                    else:
                        part = kept[t, at + i, q] * value
                        tops[i] = part if q == 0 else tops[i] + part
                        if i == size - 1:
                            part = kept_low[t, g * blocks + n, q] * value
                            low = part if q == 0 else low + part
                    value = emit[t, at + i, q] * value
                state_b[t, q] = value
            if score:
                put_sums(t, g, n, tops, low)
            return after

        def score_waiting(g, n):
            at = g * slots + n * size
            end = n * size + size - 1
            for t in team:
                tops, low = [None] * size, None
                for q in range(vecs):
                    for i in range(size):
                        part = kept[t, at + i, q] * waiting[t, n * size + i, q]
                        tops[i] = part if q == 0 else tops[i] + part
                    part = kept_low[t, g * blocks + n, q] * waiting[t, end, q]
                    low = part if q == 0 else low + part
                put_sums(t, g, n, tops, low)

        row_at = lax.broadcasted_iota(jnp.int32, (slots, LANE), 0)
        own_lane = (lax.broadcasted_iota(jnp.int32, (slots, LANE), 1) == row_at) & (row_at < local_m)

        def finish(g):
            result = jnp.zeros((SUB, LANE), jnp.float32)
            for t in team:
                def gathered(sums):
                    parts = [sums[t, pl.ds(g * slots * SUB + k, slots, stride=SUB), :] for k in range(SUB)]
                    return jnp.sum(total(parts), axis=1, keepdims=True)

                value = jnp.broadcast_to(gathered(numer) / gathered(denom), (slots, LANE))
                value = jnp.sum(jnp.where(own_lane, value, 0.0), axis=0, keepdims=True)
                result = jnp.where(sub_at == first + t, jnp.broadcast_to(value, (SUB, LANE)), result)
            dos[g] = result
            pl.when(g != g_me)(lambda: out_copy(g, g_me).start())

        for load in loads[3:]:
            load.wait()
        scale_a = arrange(0, state_a)
        scale_b = arrange(1, state_b)
        table[2 * each, end_row:end_row + SUB, :] = jnp.zeros((SUB, LANE), jnp.float32)

        def first_pass(g, scale):
            arrived(g)
            expand(g)
            read_meta(g)
            make_spans(g)
            for n in range(blocks):
                scale = step_a(g, n, scale, True)
            return scale

        scale_a = lax.fori_loop(0, far, first_pass, scale_a)
        arrived(far)
        expand(far)
        read_meta(far)
        make_spans(far)
        ready = set()
        for n in range(blocks):
            m = blocks - 1 - n
            if m != n and m not in ready:
                prepare(far, m)
            scale_a = step_a(far, n, scale_a, n not in ready)
            ready |= {n, m}
            sums = [ahead(t, state_b, far, m, down) for t in team]
            scale_b = tuple(step_b(t, far, m, scale_b[t], sums[t], False) for t in team)

        sums = ahead(0, state_b, far - 1, blocks - 1, down)
        for n in range(blocks):
            score_waiting(far, n)

        def second_pass(k, carry):
            g = far - 1 - k
            scale, sums = list(carry[0]), list(carry[1])
            for n in reversed(range(blocks)):
                scale[0] = step_b(0, g, n, scale[0], sums, True)
                if n:
                    sums = ahead(0, state_b, g, n - 1, down)
                elif groups > 4 or g > 0:
                    sums = ahead(0, state_b, jnp.maximum(g - 1, 0) if groups > 4 else g - 1, blocks - 1, down)
                for t in range(1, each):
                    scale[t] = step_b(t, g, n, scale[t], ahead(t, state_b, g, n, down), True)
                if n + 1 == blocks:
                    finish(g + 1)
            return tuple(scale), tuple(sums)

        carry = scale_b, tuple(sums)
        if groups <= 4:
            for k in range(far):
                carry = second_pass(k, carry)
        else:
            lax.fori_loop(0, far, second_pass, carry)
        finish(0)
        out_recv[g_me] = dos[g_me]

    if len(set(split)) == 1:
        pl.when(active)(lambda: run(g_me * split[0], split[0]))
    else:
        for g in range(teams):
            pl.when(g_me == g)(functools.partial(run, sum(split[:g]), split[g]))

    each_send(lambda copy: copy.wait_send())
    for g in range(teams):
        pl.when(g != g_me)(lambda: out_copy(g_me, g).wait_recv())
    result = out_recv[0]
    for g in range(1, teams):
        result = jnp.where(sub_at >= sum(split[:g]), out_recv[g], result)
    out[...] = result[0:targets, 0:local_m]

    @pl.when(active)
    def _():
        each_group(lambda g: pl.when(g != g_me)(lambda: out_copy(g, g_me).wait_send()))


def solution(mesh):
    groups, haps = mesh.shape["grp"], mesh.shape["hap"]

    def local(alleles, observed, map_steps, start_weights, end_weights):
        local_m, local_w = alleles.shape
        targets, total_haps = start_weights.shape
        words = local_w * haps
        bits_word = total_haps // words
        reps = LANE * SUB // words
        vecs = bits_word // reps
        pack = LANE // local_w
        slots = pack * -(-local_m // pack)
        size = block_size(local_m)
        blocks = groups * (local_m // size)
        split = split_targets(targets, groups * slots * total_haps * 4)
        each, teams = max(split), len(split)
        assert targets < SUB and teams <= groups and slots % SUB == 0
        dims = (groups, haps, local_m, targets, words, bits_word)
        f32, i32 = jnp.float32, jnp.int32
        dma = pltpu.SemaphoreType.DMA
        tile = (SUB, LANE)
        out = pl.pallas_call(
            functools.partial(kernel, dims),
            out_shape=pltpu.VMEM((targets, local_m), f32),
            in_specs=[pl.BlockSpec(memory_space=pltpu.HBM)] * 5,
            out_specs=pl.BlockSpec(memory_space=pltpu.VMEM),
            scratch_shapes=[
                pltpu.VMEM((local_m, local_w), i32),
                pltpu.VMEM((targets, local_m), i32),
                pltpu.SMEM((local_m,), i32),
                pltpu.VMEM((slots + SUB, LANE), i32),
                pltpu.VMEM(tile, i32),
                pltpu.VMEM(tile, i32),
                pltpu.VMEM((groups, haps * SUB, LANE), i32),
                pltpu.VMEM((groups, *tile), i32),
                pltpu.VMEM((groups * slots, *tile), i32),
                pltpu.VMEM((2 * each + 1, groups * slots + (size + 1) * SUB, LANE), f32),
                pltpu.VMEM((2, targets, total_haps), f32),
                pltpu.VMEM((vecs * SUB * targets, LANE), f32),
                pltpu.VMEM((each, vecs, *tile), f32),
                pltpu.VMEM((each, vecs, *tile), f32),
                pltpu.VMEM((each, groups * slots, vecs, *tile), f32),
                pltpu.VMEM((each, groups, size * (size + 1) // 2, *tile), f32),
                pltpu.VMEM((each, groups * slots, vecs, *tile), f32),
                pltpu.VMEM((each, blocks, vecs, *tile), f32),
                pltpu.VMEM((each, local_m, vecs, *tile), f32),
                pltpu.VMEM((each, groups * slots * SUB, LANE), f32),
                pltpu.VMEM((each, groups * slots * SUB, LANE), f32),
                pltpu.VMEM((groups, *tile), f32),
                pltpu.VMEM((teams, *tile), f32),
                dma((5,)), dma((teams, haps)), dma((groups, haps)), dma((teams,)), dma((groups,)),
                dma((groups,)), dma((teams,)),
            ],
            compiler_params=pltpu.CompilerParams(
                collective_id=0, has_side_effects=True, vmem_limit_bytes=60 * 1024 * 1024),
        )(alleles, observed.T, map_steps, start_weights, end_weights)
        return out.T

    in_specs = (P("grp", "hap"), P("grp", "hap"), P("grp"), P("hap", None), P("hap", None))
    return jax.shard_map(local, mesh=mesh, in_specs=in_specs, out_specs=P("grp", "hap"), check_vma=False)
```

time: 19.5 us -> 18.1 us (0.928)
  Pallas kernels: 18.7 us -> 17.3 us
    pallas_call x1, Pallas kernels: 18.7 us -> 17.3 us  [local(): pl.pallas_call(functools.partial(kernel, dims), out_shape=pltpu.VMEM((tar...]
where the time goes in v4:
time: 18.1 us; the launch traced here: 17.9 us
  Pallas kernels  17.3 us (96%)
  local copies, waits for them, and re-layouts  0.58 us (3%)
    pallas_call x1, Pallas kernels, local(): pl.pallas_call(functools.partial(kernel, dims), out_shape=pltpu.VMEM((tar...  17.3 us
    unnamed x1, local copies, waits for them, and re-layouts  0.58 us

profile of v4, /device:TPU:0, one launch (start us, length us, event | category | flops | bytes accessed | tf_op | source)
XLA Modules:
  0.0 17.9 jit_solution(12320910388519664765)
XLA Ops:
  0.0 17.3 %shard_map.55 = f32[4,15]{1,0:T(4,128)S(1)} custom-call(s32[15,64]{1,0:T(8,128)} %alleles.1, s32[4,15]{1,0:T(4,128)} %bitcast.3, s32[15]{0:T(128)} %steps.1, f32[4,15360]{1,0:T(4,128)} %starts.1, f32[4,15360]{1,0:T(4,128)} %ends.1), custom_call_target="tpu_custom_call" | custom-call | tf_op jit(solution)/shard_map/pallas_call | solution.py:477
  17.3 0.6 %copy.7 = f32[15,4]{0,1:T(4,128)} copy(f32[15,4]{0,1:T(4,128)S(1)} %bitcast.2) | data formatting | bytes 480

commit v5 on v4

--- a/solution.py
+++ b/solution.py
@@ -67,10 +67,10 @@
 
     def each_group(act):
         if groups <= 4:
-            for g in reversed(range(groups)):
+            for g in range(groups):
                 act(g)
         else:
-            pl.loop(0, groups)(lambda k: act(far - k))
+            pl.loop(0, groups)(act)
 
     def not_me(g, h, act):
         pl.when((g != g_me) | (h != h_me))(act)
@@ -155,8 +155,10 @@
                     sums[t] = value[t] if q == 0 else sums[t] + value[t]
             return tuple(1.0 / add_up(sums[t]) for t in range(each))
 
+        def meta_arrived(g):
+            pl.when(g != g_me)(lambda: meta_copy(g_me, g).wait_recv())
+
         def arrived(g):
-            pl.when(g != g_me)(lambda: meta_copy(g_me, g).wait_recv())
             each_hap(lambda h: not_me(g, h, lambda: block_copy(g_me, h_me, g, h).wait_recv()))
 
         def read_meta(g):
@@ -204,13 +206,13 @@
         def prepare(g, n):
             at = g * slots + n * size
             words_in = [bits[at + i] for i in range(size)]
-            for t in team:
-                tops = [(row(2 * t, at + i), row(2 * t + 1, at + i)) for i in range(size)]
-                for q in range(vecs):
-                    for i in range(size):
-                        mask = masked(words_in[i], q)
-                        emit[t, at + i, q] = jnp.where(mask, *tops[i])
-                        kept[t, at + i, q] = jnp.where(mask, tops[i][0], 0.0)
+            tops = [[(row(2 * t, at + i), row(2 * t + 1, at + i)) for i in range(size)] for t in team]
+            for q in range(vecs):
+                for i in range(size):
+                    mask = masked(words_in[i], q)
+                    for t in team:
+                        emit[t, at + i, q] = jnp.where(mask, *tops[t][i])
+                        kept[t, at + i, q] = jnp.where(mask, tops[t][i][0], 0.0)
 
         inner = min(size, 4)
         used = sum(1 << (reps * q) for q in range(vecs))
@@ -287,26 +289,9 @@
 
         up, down = list(range(size)), list(range(size))[::-1]
 
-        def prepare_ahead(g, n):
+        def step_a(g, n, scale):
             at = g * slots + n * size
-            words_in = [bits[at + i] for i in range(size)]
-            sums = [[None] * size for t in team]
-            tops = [[(row(2 * t, at + i), row(2 * t + 1, at + i)) for i in range(size)] for t in team]
-            for q in range(vecs):
-                masks = [masked(words_in[i], q) for i in range(size)]
-                for t in team:
-                    value = state_a[t, q]
-                    for i in up:
-                        e = jnp.where(masks[i], *tops[t][i])
-                        emit[t, at + i, q] = e
-                        kept[t, at + i, q] = jnp.where(masks[i], tops[t][i][0], 0.0)
-                        value = value * e
-                        sums[t][i] = value if q == 0 else sums[t][i] + value
-            return [[add_up(value) for value in sums[t]] for t in team]
-
-        def step_a(g, n, scale, fresh):
-            at = g * slots + n * size
-            sums = prepare_ahead(g, n) if fresh else [ahead(t, state_a, g, n, up) for t in team]
+            sums = [ahead(t, state_a, g, n, up) for t in team]
             solved = [solve(t, sums[t], scale[t], g, n, up, False) for t in team]
             for t in team:
                 for q in range(vecs):
@@ -383,26 +368,29 @@
         table[2 * each, end_row:end_row + SUB, :] = jnp.zeros((SUB, LANE), jnp.float32)
 
         def first_pass(g, scale):
+            meta_arrived(g)
             arrived(g)
             expand(g)
             read_meta(g)
             make_spans(g)
             for n in range(blocks):
-                scale = step_a(g, n, scale, True)
+                prepare(g, n)
+                scale = step_a(g, n, scale)
             return scale
 
         scale_a = lax.fori_loop(0, far, first_pass, scale_a)
+        meta_arrived(far)
+        read_meta(far)
         arrived(far)
         expand(far)
-        read_meta(far)
         make_spans(far)
         ready = set()
         for n in range(blocks):
             m = blocks - 1 - n
-            if m != n and m not in ready:
-                prepare(far, m)
-            scale_a = step_a(far, n, scale_a, n not in ready)
+            for k in sorted({n, m} - ready):
+                prepare(far, k)
             ready |= {n, m}
+            scale_a = step_a(far, n, scale_a)
             sums = [ahead(t, state_b, far, m, down) for t in team]
             scale_b = tuple(step_b(t, far, m, scale_b[t], sums[t], False) for t in team)
 

time: 18.1 us -> 17.9 us (0.989)
  Pallas kernels: 17.3 us -> 17.1 us
    pallas_call x1, Pallas kernels: 17.3 us -> 17.1 us  [local(): pl.pallas_call(functools.partial(kernel, dims), out_shape=pltpu.VMEM((tar...]
where the time goes in v5:
time: 17.9 us; the launch traced here: 17.7 us
  Pallas kernels  17.1 us (96%)
  local copies, waits for them, and re-layouts  0.58 us (3%)
    pallas_call x1, Pallas kernels, local(): pl.pallas_call(functools.partial(kernel, dims), out_shape=pltpu.VMEM((tar...  17.1 us
    unnamed x1, local copies, waits for them, and re-layouts  0.58 us

profile of v5, /device:TPU:0, one launch (start us, length us, event | category | flops | bytes accessed | tf_op | source)
XLA Modules:
  0.0 17.7 jit_solution(2303401612945629184)
XLA Ops:
  0.0 17.1 %shard_map.55 = f32[4,15]{1,0:T(4,128)S(1)} custom-call(s32[15,64]{1,0:T(8,128)} %alleles.1, s32[4,15]{1,0:T(4,128)} %bitcast.3, s32[15]{0:T(128)} %steps.1, f32[4,15360]{1,0:T(4,128)} %starts.1, f32[4,15360]{1,0:T(4,128)} %ends.1), custom_call_target="tpu_custom_call" | custom-call | tf_op jit(solution)/shard_map/pallas_call | solution.py:465
  17.1 0.6 %copy.7 = f32[15,4]{0,1:T(4,128)} copy(f32[15,4]{0,1:T(4,128)S(1)} %bitcast.2) | data formatting | bytes 480

commit v6 on v5

--- a/solution.py
+++ b/solution.py
@@ -367,11 +367,14 @@
         scale_b = arrange(1, state_b)
         table[2 * each, end_row:end_row + SUB, :] = jnp.zeros((SUB, LANE), jnp.float32)
 
+        meta_arrived(0)
+        read_meta(0)
+
         def first_pass(g, scale):
-            meta_arrived(g)
             arrived(g)
+            meta_arrived(g + 1)
             expand(g)
-            read_meta(g)
+            read_meta(g + 1)
             make_spans(g)
             for n in range(blocks):
                 prepare(g, n)
@@ -379,8 +382,6 @@
             return scale
 
         scale_a = lax.fori_loop(0, far, first_pass, scale_a)
-        meta_arrived(far)
-        read_meta(far)
         arrived(far)
         expand(far)
         make_spans(far)

time: 17.9 us -> 17.8 us (level)
  no operation moved by 1% of the time
where the time goes in v6:
time: 17.8 us; the launch traced here: 17.6 us
  Pallas kernels  17 us (96%)
  local copies, waits for them, and re-layouts  0.58 us (3%)
    pallas_call x1, Pallas kernels, local(): pl.pallas_call(functools.partial(kernel, dims), out_shape=pltpu.VMEM((tar...  17 us
    unnamed x1, local copies, waits for them, and re-layouts  0.58 us

profile of v6, /device:TPU:0, one launch (start us, length us, event | category | flops | bytes accessed | tf_op | source)
XLA Modules:
  0.0 17.6 jit_solution(17834544109495762225)
XLA Ops:
  0.0 17.0 %shard_map.55 = f32[4,15]{1,0:T(4,128)S(1)} custom-call(s32[15,64]{1,0:T(8,128)} %alleles.1, s32[4,15]{1,0:T(4,128)} %bitcast.3, s32[15]{0:T(128)} %steps.1, f32[4,15360]{1,0:T(4,128)} %starts.1, f32[4,15360]{1,0:T(4,128)} %ends.1), custom_call_target="tpu_custom_call" | custom-call | tf_op jit(solution)/shard_map/pallas_call | solution.py:466
  17.0 0.6 %copy.7 = f32[15,4]{0,1:T(4,128)} copy(f32[15,4]{0,1:T(4,128)S(1)} %bitcast.2) | data formatting | bytes 480
